TPU v7x, 256 devices: a whole 4x4x8 slice. The times are simulated.
256 devices in a mesh: seq: 128 (over y, z_hi, x, core), ch: 2 (over z_lo).
Axes of the slice: x: 4, y: 4, z: 8 (z_hi: 4, z_lo: 2; z = z_hi * 2 + z_lo), core: 2. Of those that a mesh axis runs over, the one named last changes fastest.
Arguments:
- tokens: bfloat16 [16384, 8192], P('seq', 'ch'), may hold values from -6 to 6
- query_in: bfloat16 [16384, 8192], P('seq', 'ch'), may hold values from -6 to 6
- key_in: bfloat16 [16384, 8192], P('seq', 'ch'), may hold values from -6 to 6
- proj_in: bfloat16 [8192, 1536], P('ch', 'seq'), may hold values from -0.0625 to 0.0625
- proj_out: bfloat16 [1536, 8192], P('seq', 'ch'), may hold values from -0.15625 to 0.15625
- short_taps: float32 [3, 7, 8192], P(None, None, 'ch'), may hold values from -2.4 to 2.4
- residues: float32 [16, 8192], P(None, 'ch'), may hold values from -1.8 to 1.8
- mode_rates: float32 [16, 8192], P(None, 'ch'), may hold values from 3.0517578e-05 to 0.03
- skip_gain: float32 [8192], P('ch'), may hold values from -3 to 3
Outputs:
- operator_out: bfloat16 [16384, 8192], P('seq', 'ch')
All inputs are finite; a program needn't handle non-finite values.
Results may differ from a plain program's by a relative error of at most 0.0069.
Values may be sent and summed in bfloat16 or wider, within the bound.
A program may use at most 192 MiB of HBM per device.

v0:
```python
import jax
import jax.numpy as jnp
from jax import lax
from jax.experimental import pallas as pl
from jax.experimental.pallas import tpu as pltpu
from jax.sharding import Mesh
from jax.sharding import PartitionSpec as P

ROWS = 128
WIDE = 4096
LANES = 128
TILES = WIDE // LANES
GROUPS = TILES // 8
MODES = 16
TAPS = 7
SEQ_AXES = ("y", "zh", "x", "core")


def spread(source, edge, scratch):
    for tile in range(TILES):
        columns = slice(tile * LANES, (tile + 1) * LANES)
        scratch[tile * 8 : tile * 8 + 8, :] = edge[:, columns]

    @pl.loop(0, ROWS // 16)
    def _(pair):
        for tile in range(TILES):
            columns = slice(tile * LANES, (tile + 1) * LANES)
            block = source[pl.ds(pl.multiple_of(pair * 16, 16), 16), columns].astype(jnp.float32)
            base = pl.multiple_of((2 * pair + 1) * TILES * 8 + tile * 8, 8)
            scratch[pl.ds(base, 8), :] = block[:8]
            scratch[pl.ds(base + TILES * 8, 8), :] = block[8:]


def row_of(scratch, eight, group, row):
    start = (eight + (1 if row >= 0 else 0)) * TILES * 8 + group * 64 + row % 8
    return scratch[pl.ds(start, 8, stride=8), :]


def short(rows, taps, step):
    result = taps[0] * rows[step + 6]
    for offset in range(1, TAPS):
        result = result + taps[offset] * rows[step + 6 - offset]
    return result


def mix_kernel(key, value, key_edge, value_edge, taps, decay, mixed, state, key_rows, value_rows):
    spread(key, key_edge, key_rows)
    spread(value, value_edge, value_rows)
    for group in range(GROUPS):
        key_taps = [taps[1, j, group] for j in range(TAPS)]
        value_taps = [taps[2, j, group] for j in range(TAPS)]

        @pl.loop(0, ROWS // 8)
        def _(eight):
            keys = [row_of(key_rows, eight, group, r) for r in range(-6, 8)]
            values = [row_of(value_rows, eight, group, r) for r in range(-6, 8)]
            for step in range(8):
                product = short(keys, key_taps, step) * short(values, value_taps, step)
                product = product.astype(jnp.bfloat16).astype(jnp.float32)
                mixed[eight * 8 + step, group * 8 : group * 8 + 8, :] = product

    for group in range(GROUPS):
        rates = [decay[n, group] for n in range(MODES)]

        def advance(eight, held):
            held = list(held)
            for step in range(8):
                entry = mixed[eight * 8 + step, group * 8 : group * 8 + 8, :]
                held = [rates[n] * held[n] + entry for n in range(MODES)]
            return tuple(held)

        held = lax.fori_loop(
            0, ROWS // 8, advance, (jnp.zeros((8, LANES), jnp.float32),) * MODES
        )
        for n in range(MODES):
            state[pl.ds(group * 128 + n, 8, stride=16), :] = held[n]


def scan_kernel(arrived, decay, before):
    rate = decay[...]

    def advance(block, held):
        before[block] = held
        return rate * held + arrived[block]

    lax.fori_loop(0, arrived.shape[0], advance, jnp.zeros(rate.shape, jnp.float32))


def out_kernel(query, query_edge, mixed, state, taps, decay, weight, skip, out, query_rows, out_rows):
    spread(query, query_edge, query_rows)
    for group in range(GROUPS):
        rates = [decay[n, group] for n in range(MODES)]
        weights = [weight[n, group] for n in range(MODES)]

        def advance(eight, held):
            held = list(held)
            for step in range(8):
                entry = mixed[eight * 8 + step, group * 8 : group * 8 + 8, :]
                held = [rates[n] * held[n] + entry for n in range(MODES)]
                terms = [weights[n] * held[n] for n in range(MODES)]
                while len(terms) > 1:
                    terms = [terms[i] + terms[i + 1] for i in range(0, len(terms), 2)]
                start = eight * TILES * 8 + group * 64 + step
                out_rows[pl.ds(start, 8, stride=8), :] = terms[0]
            return tuple(held)

        first = tuple(state[pl.ds(group * 128 + n, 8, stride=16), :] for n in range(MODES))
        lax.fori_loop(0, ROWS // 8, advance, first)

    for group in range(GROUPS):
        query_taps = [taps[0, j, group] for j in range(TAPS)]
        skip_part = skip[group]

        @pl.loop(0, ROWS // 8)
        def _(eight):
            queries = [row_of(query_rows, eight, group, r) for r in range(-6, 8)]
            for step in range(8):
                entry = mixed[eight * 8 + step, group * 8 : group * 8 + 8, :]
                start = eight * TILES * 8 + group * 64 + step
                convolved = out_rows[pl.ds(start, 8, stride=8), :]
                convolved = convolved.astype(jnp.bfloat16).astype(jnp.float32)
                out_rows[pl.ds(start, 8, stride=8), :] = short(queries, query_taps, step) * (
                    convolved + skip_part * entry
                )

    @pl.loop(0, ROWS // 16)
    def _(pair):
        for tile in range(TILES):
            base = pl.multiple_of(2 * pair * TILES * 8 + tile * 8, 8)
            block = jnp.concatenate(
                [out_rows[pl.ds(base, 8), :], out_rows[pl.ds(base + TILES * 8, 8), :]], axis=0
            )
            out[pl.ds(pl.multiple_of(pair * 16, 16), 16), tile * LANES : (tile + 1) * LANES] = (
                block.astype(jnp.bfloat16)
            )


def grouped(value):
    return value.reshape(*value.shape[:-1], GROUPS, 8, LANES)


def long_part(query_in, key_in, value_proj, edges, short_taps, residues, mode_rates, skip_gain):
    f32 = jnp.float32
    rows_scratch = pltpu.VMEM(((ROWS + 8) * TILES, LANES), f32)
    taps = grouped(short_taps)
    decay = grouped(jnp.exp(-mode_rates))
    weight = grouped(residues * jnp.sqrt(mode_rates))
    mixed, state = pl.pallas_call(
        mix_kernel,
        out_shape=(
            jax.ShapeDtypeStruct((ROWS, TILES, LANES), f32),
            jax.ShapeDtypeStruct((TILES * MODES, LANES), f32),
        ),
        scratch_shapes=[rows_scratch, rows_scratch],
        compiler_params=pltpu.CompilerParams(vmem_limit_bytes=40 * 2**20),
    )(key_in, value_proj, edges[1], edges[2], taps, decay)
    seq = 128
    sent = state.reshape(seq, 4, LANES)
    arrived = lax.all_to_all(sent, SEQ_AXES, split_axis=0, concat_axis=0, tiled=True)
    me = lax.axis_index(SEQ_AXES)
    mine = lax.dynamic_slice(mode_rates, (me % 4 * 4, me // 4 * LANES), (4, LANES))
    before = pl.pallas_call(
        scan_kernel, out_shape=jax.ShapeDtypeStruct((seq, 4, LANES), f32)
    )(arrived, jnp.exp(-ROWS * mine))
    first = lax.all_to_all(before, SEQ_AXES, split_axis=0, concat_axis=0, tiled=True)
    return pl.pallas_call(
        out_kernel,
        out_shape=jax.ShapeDtypeStruct((ROWS, WIDE), jnp.bfloat16),
        scratch_shapes=[rows_scratch, pltpu.VMEM((ROWS * TILES, LANES), f32)],
        compiler_params=pltpu.CompilerParams(vmem_limit_bytes=40 * 2**20),
    )(
        query_in,
        edges[0],
        mixed,
        first.reshape(TILES * MODES, LANES),
        taps,
        decay,
        weight,
        grouped(skip_gain),
    )


def value_part(tokens, proj_in, proj_out):
    f32 = jnp.float32
    places = ("y", "zh", "x")
    swap = [(0, 1), (1, 0)]
    other_tokens = lax.ppermute(tokens, "core", swap)
    in_rows = lax.all_gather(proj_in.T, places, axis=0, tiled=True)
    out_rows = lax.all_gather(proj_out, places, axis=0, tiled=True)
    contract = (((1,), (1,)), ((), ()))
    chip_tokens = jnp.concatenate([tokens, other_tokens], axis=0)
    partial = lax.dot_general(chip_tokens, in_rows, contract, preferred_element_type=f32)
    other = lax.ppermute(partial, "ch", swap)
    low_rank = (partial + other).astype(jnp.bfloat16)
    sent = jnp.dot(low_rank[ROWS:], out_rows, preferred_element_type=f32)
    arrived = lax.ppermute(sent, "core", swap)
    kept = jnp.dot(low_rank[:ROWS], out_rows, preferred_element_type=f32)
    return (kept + arrived).astype(jnp.bfloat16)


def per_device(
    tokens, query_in, key_in, proj_in, proj_out, short_taps, residues, mode_rates, skip_gain
):
    value_proj = value_part(tokens, proj_in, proj_out)
    ring = [(i, i + 1) for i in range(127)]
    margin = TAPS - 1

    def edge_of(last):
        edge = lax.ppermute(last, SEQ_AXES, ring)
        return jnp.pad(edge.astype(jnp.float32), ((0, 0), (2, 0), (0, 0)))

    early = edge_of(jnp.stack([query_in[ROWS - margin :], key_in[ROWS - margin :]]))
    late = edge_of(value_proj[None, ROWS - margin :])
    edges = (early[0], early[1], late[0])
    return long_part(
        query_in, key_in, value_proj, edges, short_taps, residues, mode_rates, skip_gain
    )


def solution(mesh):
    split = Mesh(mesh.devices.reshape(4, 4, 4, 2, 2), ("y", "zh", "x", "core", "ch"))
    both = P(SEQ_AXES, "ch")
    placed = (
        both,
        both,
        both,
        P("ch", SEQ_AXES),
        both,
        P(None, None, "ch"),
        P(None, "ch"),
        P(None, "ch"),
        P("ch"),
    )
    return jax.shard_map(
        per_device, mesh=split, in_specs=placed, out_specs=both, check_vma=False
    )
```

profile of v0, /device:TPU:1, one launch (start us, length us, event | category | flops | bytes accessed | tf_op | source)
XLA Modules:
  0.0 360.5 jit_solution(12299858525277152895)
XLA Ops:
  8.0 3.3 collective-permute-start.1
  11.3 110.3 %all-gather.5.cloned.1.call-done = bf16[64,12,4096]{2,1,0:T(8,128)(2,1)} async-done(((bf16[1,12,4096]{2,1,0:T(8,128)(2,1)}), bf16[64,12,4096]{2,1,0:T(8,128)(2,1)}) %all-gather.5.cloned.1.call-update) | async-done | bytes 6291472 | tf_op jit(solution)/shard_map/all_gather | solution.py:188
  121.6 9.8 %reshape.26 = bf16[768,4096]{1,0:T(8,128)(2,1)} reshape(bf16[64,12,4096]{2,1,0:T(8,128)(2,1)} %all-gather.5.cloned.1.call-done) | data formatting | bytes 12582912
  131.5 4.9 %fusion.1 = f32[256,768]{1,0:T(8,128)S(1)} fusion(bf16[768,4096]{1,0:T(8,128)(2,1)} %reshape.26, bf16[128,4096]{1,0:T(8,128)(2,1)} %collective-permute-done.1, bf16[128,4096]{1,0:T(8,128)(2,1)S(1)} %copy-done.7), kind=kOutput, calls=%fused_computation.2 | convolution fusion | flops 1614807040 | bytes 9175040 | tf_op jit(solution)/shard_map/dot_general | solution.py:192
  136.4 8.9 %collective-permute-start.2 = (f32[256,768]{1,0:T(8,128)S(1)}, f32[256,768]{1,0:T(8,128)S(1)}, u32[]{:S(2)}, u32[]{:S(2)}) collective-permute-start(f32[256,768]{1,0:T(8,128)S(1)} %fusion.1), channel_id=1, source_target_pairs={{0,1},{1,0},{2,3},{3,2},{4,5},{5,4},{6,7},{7,6},{8,9},{9,8},{10,11... | collective-permute-start | bytes 2359304 | tf_op jit(solution)/shard_map/ppermute | solution.py:193
  145.3 93.8 %all-gather.7.cloned.1.call-done = bf16[64,12,4096]{2,1,0:T(8,128)(2,1)} async-done(((bf16[1,12,4096]{2,1,0:T(8,128)(2,1)}), bf16[64,12,4096]{2,1,0:T(8,128)(2,1)}) %all-gather.7.cloned.1.call-update) | async-done | bytes 6291472 | tf_op jit(solution)/shard_map/all_gather | solution.py:189
  239.0 9.9 %reshape.28 = bf16[768,4096]{1,0:T(8,128)(2,1)} reshape(bf16[64,12,4096]{2,1,0:T(8,128)(2,1)} %all-gather.7.cloned.1.call-done) | data formatting | bytes 12582912
  249.0 3.8 %fusion.5 = f32[128,4096]{1,0:T(8,128)S(1)} fusion(bf16[768,4096]{1,0:T(8,128)(2,1)} %reshape.28, bf16[256,768]{1,0:T(8,128)(2,1)S(1)} %add_convert_fusion), kind=kOutput, calls=%fused_computation.9 | convolution fusion | flops 805306368 | bytes 8585216 | tf_op jit(solution)/shard_map/dot_general | solution.py:195
  252.9 8.5 %collective-permute-start.3 = (f32[128,4096]{1,0:T(8,128)S(1)}, f32[128,4096]{1,0:T(8,128)}, u32[]{:S(2)}, u32[]{:S(2)}) collective-permute-start(f32[128,4096]{1,0:T(8,128)S(1)} %fusion.5), channel_id=1, source_target_pairs={{0,2},{2,0},{1,3},{3,1},{4,6},{6,4},{5,7},{7,5},{8,10},{10,8},{9,1... | collective-permute-start | bytes 6291464 | tf_op jit(solution)/shard_map/ppermute | solution.py:196
  263.0 1.9 collective-permute-start
  266.0 1.2 collective-permute-done
  268.1 4.5 %fusion.value = bf16[128,4096]{1,0:T(8,128)(2,1)S(1)} fusion(f32[128,4096]{1,0:T(8,128)} %collective-permute-done.3, bf16[768,4096]{1,0:T(8,128)(2,1)} %reshape.28, bf16[256,768]{1,0:T(8,128)(2,1)S(1)} %add_convert_fusion), kind=kOutput, calls=%fused_computation.1 | convolution fusion | flops 806354944 | bytes 9633792 | tf_op jit(solution)/shard_map/dot_general | solution.py:197
  272.7 4.4 %collective-permute-start.4 = (bf16[1,6,4096]{2,1,0:T(8,128)(2,1)S(1)}, bf16[1,6,4096]{2,1,0:T(8,128)(2,1)S(1)}, u32[]{:S(2)}, u32[]{:S(2)}) collective-permute-start(bf16[1,6,4096]{2,1,0:T(8,128)(2,1)S(1)} %slice_bitcast_fusion.2), channel_id=1, source_target_pairs={{0,2},{2,4},{4,6},{6,8},{8,10},{10,12},{12,14},{14,16},{16,18},{18... | collective-permute-start | bytes 147464 | tf_op jit(solution)/shard_map/ppermute | solution.py:209
  277.1 1.3 collective-permute-done.4
  278.4 6.5 %shard_map.91 = (f32[128,32,128]{2,1,0:T(8,128)S(1)}, f32[512,128]{1,0:T(8,128)}) custom-call(bf16[128,4096]{1,0:T(8,128)(2,1)S(1)} %copy-done, bf16[128,4096]{1,0:T(8,128)(2,1)S(1)} %fusion.value, f32[8,4096]{1,0:T(8,128)S(1)} %get-tuple-element.11.key_edge, f32[8,4096]{1,0:T(8,128)S(1)} %bitcast_convert_fusion.value_edge, ...), custom_call_target="tpu_custom_call" | custom-call | tf_op jit(solution)/shard_map/pallas_call | solution.py:148
  284.9 19.4 %all-to-all-start = ((f32[128,4,128]{2,1,0:T(4,128)}), f32[128,4,128]{2,1,0:T(4,128)S(1)}, u32[]{:S(2)}, u32[]{:S(2)}) async-start(f32[128,4,128]{2,1,0:T(4,128)} %bitcast.9), calls=%async_computation | async-start | bytes 524288 | tf_op jit(solution)/shard_map/all_to_all | solution.py:159
  304.3 1.3 multiply_exponential_fusion.decay
  305.7 14.0 %all-to-all-done.arrived = f32[128,4,128]{2,1,0:T(4,128)S(1)} async-done(((f32[128,4,128]{2,1,0:T(4,128)}), f32[128,4,128]{2,1,0:T(4,128)S(1)}, u32[]{:S(2)}, u32[]{:S(2)}) %all-to-all-start) | async-done | bytes 262176 | tf_op jit(solution)/shard_map/all_to_all | solution.py:159
  320.4 2.4 shard_map.92
  322.8 6.6 %all-to-all-start.1 = ((f32[128,4,128]{2,1,0:T(4,128)}), f32[128,4,128]{2,1,0:T(4,128)S(1)}, u32[]{:S(2)}, u32[]{:S(2)}) async-start(f32[128,4,128]{2,1,0:T(4,128)} %shard_map.92), calls=%async_computation.1 | async-start | bytes 524288 | tf_op jit(solution)/shard_map/all_to_all | solution.py:165
  329.4 1.0 copy.11
  330.4 14.1 %all-to-all-done.1 = f32[128,4,128]{2,1,0:T(4,128)S(1)} async-done(((f32[128,4,128]{2,1,0:T(4,128)}), f32[128,4,128]{2,1,0:T(4,128)S(1)}, u32[]{:S(2)}, u32[]{:S(2)}) %all-to-all-start.1) | async-done | bytes 262176 | tf_op jit(solution)/shard_map/all_to_all | solution.py:165
  344.5 1.2 copy-done.1
  345.7 8.0 %shard_map.93 = bf16[128,4096]{1,0:T(8,128)(2,1)} custom-call(bf16[128,4096]{1,0:T(8,128)(2,1)S(1)} %copy-done.1, f32[8,4096]{1,0:T(8,128)S(1)} %get-tuple-element.12.query_edge, f32[128,32,128]{2,1,0:T(8,128)S(1)} %get-tuple-element.7.mixed, f32[512,128]{1,0:T(8,128)S(1)} %bitcast.33, f32[3,7,4,8,128]{4,3,2,1,0:T(8,128)S(1)} %reshape.18.taps, ...), custom_call_target="tpu_custom_call" | custom-call | tf_op jit(solution)/shard_map/pallas_call | solution.py:166
  (32 shorter events, 5.9 us)
Async XLA Ops:
  6.5 115.1 %all-gather.5.cloned.1.call-start = ((), (), s32[]{:S(2)}) async-start(), calls=%async_computation.2 | async-start | bytes 8519680 | tf_op jit(solution)/shard_map/all_gather | solution.py:188
  7.3 231.8 %all-gather.7.cloned.1.call-start = ((), (), s32[]{:S(2)}) async-start(), calls=%async_computation.3 | async-start | bytes 8519680 | tf_op jit(solution)/shard_map/all_gather | solution.py:189
  8.0 123.5 %copy-start.7 = (bf16[128,4096]{1,0:T(8,128)(2,1)S(1)}, bf16[128,4096]{1,0:T(8,128)(2,1)}, u32[]{:S(2)}) copy-start(bf16[128,4096]{1,0:T(8,128)(2,1)} %param.9) | copy-start | bytes 3145732
  8.0 123.4 %collective-permute-start.1 = (bf16[128,4096]{1,0:T(8,128)(2,1)}, bf16[128,4096]{1,0:T(8,128)(2,1)}, u32[]{:S(2)}, u32[]{:S(2)}) collective-permute-start(bf16[128,4096]{1,0:T(8,128)(2,1)} %param.9), channel_id=1, source_target_pairs={{0,2},{2,0},{1,3},{3,1},{4,6},{6,4},{5,7},{7,5},{8,10},{10,8},{9,1... | collective-permute-start | bytes 3145736 | tf_op jit(solution)/shard_map/ppermute | solution.py:187
  136.4 112.5 %collective-permute-start.2 = (f32[256,768]{1,0:T(8,128)S(1)}, f32[256,768]{1,0:T(8,128)S(1)}, u32[]{:S(2)}, u32[]{:S(2)}) collective-permute-start(f32[256,768]{1,0:T(8,128)S(1)} %fusion.1), channel_id=1, source_target_pairs={{0,1},{1,0},{2,3},{3,2},{4,5},{5,4},{6,7},{7,6},{8,9},{9,8},{10,11... | collective-permute-start | bytes 2359304 | tf_op jit(solution)/shard_map/ppermute | solution.py:193
  249.0 15.9 %copy-start.5 = (f32[16,4096]{1,0:T(8,128)S(1)}, f32[16,4096]{1,0:T(8,128)}, u32[]{:S(2)}) copy-start(f32[16,4096]{1,0:T(8,128)} %param.16) | copy-start | bytes 786436
  249.0 15.9 %copy-start.6 = (f32[16,4096]{1,0:T(8,128)S(1)}, f32[16,4096]{1,0:T(8,128)}, u32[]{:S(2)}) copy-start(f32[16,4096]{1,0:T(8,128)} %param.15) | copy-start | bytes 786436
  249.0 16.8 %copy-start.4 = (f32[3,7,4096]{2,1,0:T(8,128)S(1)}, f32[3,7,4096]{2,1,0:T(8,128)}, u32[]{:S(2)}) copy-start(f32[3,7,4096]{2,1,0:T(8,128)} %param.14) | copy-start | bytes 1032196
  252.9 15.3 %collective-permute-start.3 = (f32[128,4096]{1,0:T(8,128)S(1)}, f32[128,4096]{1,0:T(8,128)}, u32[]{:S(2)}, u32[]{:S(2)}) collective-permute-start(f32[128,4096]{1,0:T(8,128)S(1)} %fusion.5), channel_id=1, source_target_pairs={{0,2},{2,0},{1,3},{3,1},{4,6},{6,4},{5,7},{7,5},{8,10},{10,8},{9,1... | collective-permute-start | bytes 6291464 | tf_op jit(solution)/shard_map/ppermute | solution.py:196
  263.0 4.2 %collective-permute-start = (bf16[2,6,4096]{2,1,0:T(8,128)(2,1)}, bf16[2,6,4096]{2,1,0:T(8,128)(2,1)}, u32[]{:S(2)}, u32[]{:S(2)}) collective-permute-start(bf16[2,6,4096]{2,1,0:T(8,128)(2,1)} %pad_maximum_fusion), channel_id=1, source_target_pairs={{0,2},{2,4},{4,6},{6,8},{8,10},{10,12},{12,14},{14,16},{16,18},{18... | collective-permute-start | bytes 294920 | tf_op jit(solution)/shard_map/ppermute | solution.py:209
  268.1 10.3 %copy-start = (bf16[128,4096]{1,0:T(8,128)(2,1)S(1)}, bf16[128,4096]{1,0:T(8,128)(2,1)}, u32[]{:S(2)}) copy-start(bf16[128,4096]{1,0:T(8,128)(2,1)} %key.1) | copy-start | bytes 3145732
  272.6 71.8 %copy-start.2 = (f32[4096]{0:T(1024)S(1)}, f32[4096]{0:T(1024)}, u32[]{:S(2)}) copy-start(f32[4096]{0:T(1024)} %param.17) | copy-start | bytes 49156
  272.7 5.7 %collective-permute-start.4 = (bf16[1,6,4096]{2,1,0:T(8,128)(2,1)S(1)}, bf16[1,6,4096]{2,1,0:T(8,128)(2,1)S(1)}, u32[]{:S(2)}, u32[]{:S(2)}) collective-permute-start(bf16[1,6,4096]{2,1,0:T(8,128)(2,1)S(1)} %slice_bitcast_fusion.2), channel_id=1, source_target_pairs={{0,2},{2,4},{4,6},{6,8},{8,10},{10,12},{12,14},{14,16},{16,18},{18... | collective-permute-start | bytes 147464 | tf_op jit(solution)/shard_map/ppermute | solution.py:209
  284.9 34.8 %all-to-all-start = ((f32[128,4,128]{2,1,0:T(4,128)}), f32[128,4,128]{2,1,0:T(4,128)S(1)}, u32[]{:S(2)}, u32[]{:S(2)}) async-start(f32[128,4,128]{2,1,0:T(4,128)} %bitcast.9), calls=%async_computation | async-start | bytes 524288 | tf_op jit(solution)/shard_map/all_to_all | solution.py:159
  319.7 0.7 copy-start.3
  322.8 21.7 %all-to-all-start.1 = ((f32[128,4,128]{2,1,0:T(4,128)}), f32[128,4,128]{2,1,0:T(4,128)S(1)}, u32[]{:S(2)}, u32[]{:S(2)}) async-start(f32[128,4,128]{2,1,0:T(4,128)} %shard_map.92), calls=%async_computation.1 | async-start | bytes 524288 | tf_op jit(solution)/shard_map/all_to_all | solution.py:165
  344.5 1.2 copy-start.1
Sparse Core Ops, SparseCore 0:
  10.6 110.9 all-gather.4
  124.9 114.0 all-gather.6
where the time goes:
time: 361 us
  waiting for transfers between devices  236 us (65%)
  starting transfers between devices  53 us (15%)
  local copies, waits for them, and re-layouts  23.8 us (7%)
  Pallas kernels  16.9 us (5%)
  between operations  13.6 us (4%)
  matrix products  13.3 us (4%)
  other arithmetic  3.86 us (1%)
    all_gather x1, waiting for transfers between devices, value_part(): in_rows = lax.all_gather(proj_in.T, places, axis=0, tiled=True)  110 us
    all_gather x1, waiting for transfers between devices, value_part(): out_rows = lax.all_gather(proj_out, places, axis=0, tiled=True)  93.8 us
    unnamed x20, local copies, waits for them, and re-layouts  22.7 us
    all_to_all x1, starting transfers between devices, long_part(): lax.all_to_all(sent, SEQ_AXES, split_axis=0, concat_axis=0, tiled=True)  19.4 us
    all_to_all x1, waiting for transfers between devices, long_part(): lax.all_to_all(before, SEQ_AXES, split_axis=0, concat_axis=0, tiled=True)  14.1 us
    all_to_all x1, waiting for transfers between devices, long_part(): lax.all_to_all(sent, SEQ_AXES, split_axis=0, concat_axis=0, tiled=True)  14 us
    ppermute x1, starting transfers between devices, value_part(): other = lax.ppermute(partial, 'ch', swap)  8.86 us
    ppermute x1, starting transfers between devices, value_part(): arrived = lax.ppermute(sent, 'core', swap)  8.55 us
  transfers between devices with their start and end apart: 9, of which 6 were waited for; matrix products, arithmetic and copies ran while one was open for 8% of the time, Pallas kernels for 0%

commit v1 on v0

--- a/solution.py
+++ b/solution.py
@@ -180,22 +180,297 @@
     )
 
 
+MESH = pl.DeviceIdType.MESH
+BLOCK = 48
+QUARTER = 1024
+UNITS = ((0, 0), (1, 0), (0, 1), (0, 3), (0, 2), (1, 1), (1, 3), (1, 2))
+
+
+def value_kernel(
+    tokens,
+    pad_in,
+    pad_out,
+    value,
+    chip_tokens,
+    stage,
+    weights,
+    partial,
+    theirs,
+    low,
+    total,
+    arrived,
+    own_sem,
+    token_sems,
+    stage_send,
+    stage_recv,
+    deep_send,
+    deep_recv,
+    ring_send,
+    ring_recv,
+    part_send,
+    part_recv,
+    swap_send,
+    swap_recv,
+):
+    y, zh, x = lax.axis_index("y"), lax.axis_index("zh"), lax.axis_index("x")
+    core, ch = lax.axis_index("core"), lax.axis_index("ch")
+    place = {"x": x, "y": y}
+    pads = (pad_in, pad_out)
+    started = []
+
+    def step(position, by):
+        return lax.rem(position + by, 4)
+
+    def copy(source, target, send, recv, device):
+        return pltpu.make_async_remote_copy(
+            src_ref=source,
+            dst_ref=target,
+            send_sem=send,
+            recv_sem=recv,
+            device_id=device,
+            device_id_type=MESH,
+        )
+
+    def send(*arguments):
+        made = copy(*arguments)
+        made.start()
+        started.append(made)
+
+    barrier = pltpu.get_barrier_semaphore()
+    greeted = [{"core": 1 - core}, {"ch": 1 - ch}]
+    greeted += [{axis: step(at, by)} for axis, at in (("x", x), ("zh", zh)) for by in (1, 2, 3)]
+    greeted += [{"y": step(y, by)} for by in (1, 3)]
+    for device in greeted:
+        pl.semaphore_signal(barrier, inc=1, device_id=device, device_id_type=MESH)
+    own_copy = pltpu.make_async_copy(tokens, chip_tokens.at[0], own_sem)
+    own_copy.start()
+    pl.semaphore_wait(barrier, len(greeted))
+
+    for f in range(2):
+        for by in (1, 3, 2):
+            to = step(x, by)
+            columns = pl.ds(pl.multiple_of(to * QUARTER, QUARTER), QUARTER)
+            send(
+                pads[f].at[:, columns],
+                stage.at[f, x],
+                stage_send.at[f, by - 1],
+                stage_recv.at[f, by - 1],
+                {"x": to},
+            )
+    send(tokens, chip_tokens.at[1], token_sems.at[0], token_sems.at[1], {"core": 1 - core})
+
+    def settle(f):
+        columns = pl.ds(pl.multiple_of(x * QUARTER, QUARTER), QUARTER)
+        own = pltpu.make_async_copy(pads[f].at[:, columns], stage.at[f, x], own_sem)
+        own.start()
+        own.wait()
+        for by in (1, 3, 2):
+            came = stage.at[f, step(x, 4 - by)]
+            copy(came, came, stage_send.at[f, by - 1], stage_recv.at[f, by - 1], {"x": x}).wait_recv()
+        parts = [stage[f, i].astype(jnp.float32)[:12] for i in range(4)]
+        weights[f, y, zh, x] = jnp.concatenate(parts, axis=0).astype(jnp.bfloat16)
+
+    def send_deep(f):
+        block = weights.at[f, y, zh, x]
+        for by in (1, 3, 2):
+            send(block, block, deep_send.at[f, by - 1], deep_recv.at[f, by - 1], {"zh": step(zh, by)})
+
+    def wait_deep(f, r):
+        by = 4 - r
+        block = weights.at[f, y, step(zh, r), x]
+        copy(block, block, deep_send.at[f, by - 1], deep_recv.at[f, by - 1], {"zh": zh}).wait_recv()
+
+    def ring(unit, late):
+        f, r = UNITS[unit]
+        deep = step(zh, r)
+        across = (f + r) % 2 == 0
+        axis = "x" if across != late else "y"
+        at = place[axis]
+
+        def item(i, half=None):
+            if not late:
+                columns = slice(None) if half is None else slice(half * 512, half * 512 + 512)
+                if across:
+                    return weights.at[f, y, deep, i, :, columns]
+                return weights.at[f, i, deep, x, :, columns]
+            blocks = slice(None) if half is None else slice(half * 2, half * 2 + 2)
+            if across:
+                return weights.at[f, i, deep, blocks]
+            return weights.at[f, blocks, deep, i]
+
+        base = 4 if late else 0
+        plus, minus = step(at, 1), step(at, 3)
+
+        def out(ref, slot, to):
+            send(ref, ref, ring_send.at[unit, base + slot], ring_recv.at[unit, base + slot], {axis: to})
+
+        def landed(ref, slot):
+            copy(
+                ref, ref, ring_send.at[unit, base + slot], ring_recv.at[unit, base + slot], {axis: at}
+            ).wait_recv()
+
+        def first():
+            out(item(at), 0, plus)
+            out(item(at), 1, minus)
+
+        def forward():
+            landed(item(minus), 0)
+            out(item(minus, 0), 2, plus)
+            landed(item(plus), 1)
+            out(item(plus, 1), 3, minus)
+
+        def finish():
+            landed(item(step(at, 2), 0), 2)
+            landed(item(step(at, 2), 1), 3)
+
+        return first, forward, finish
+
+    early = [ring(unit, False) for unit in range(8)]
+    late = [ring(unit, True) for unit in range(8)]
+
+    def unit_weights(f, r, quarter):
+        return weights[f, :, step(zh, r), quarter].reshape(4 * BLOCK, QUARTER)
+
+    def project(r):
+        @pl.loop(0, 4)
+        def _(quarter):
+            columns = pl.ds(pl.multiple_of(quarter * QUARTER, QUARTER), QUARTER)
+            part = lax.dot_general(
+                chip_tokens[:, :, columns].reshape(2 * ROWS, QUARTER),
+                unit_weights(0, r, quarter),
+                (((1,), (1,)), ((), ())),
+                preferred_element_type=jnp.float32,
+            )
+
+            @pl.when(quarter == 0)
+            def _():
+                partial[r] = part
+
+            @pl.when(quarter > 0)
+            def _():
+                partial[r] += part
+
+        send(partial.at[r], theirs.at[r], part_send.at[r], part_recv.at[r], {"ch": 1 - ch})
+
+    def join(r):
+        copy(partial.at[r], theirs.at[r], part_send.at[r], part_recv.at[r], {"ch": ch}).wait_recv()
+        low[r] = (partial[r] + theirs[r]).astype(jnp.bfloat16)
+
+    def expand(r, opening, closing):
+        for quarter in range(4):
+            part = jnp.dot(
+                low[r], unit_weights(1, r, quarter), preferred_element_type=jnp.float32
+            ).reshape(2, ROWS, QUARTER)
+            if opening:
+                total[:, quarter] = part
+            else:
+                total[:, quarter] += part
+            if closing:
+                send(
+                    total.at[1, quarter],
+                    arrived.at[quarter],
+                    swap_send.at[quarter],
+                    swap_recv.at[quarter],
+                    {"core": 1 - core},
+                )
+
+    FIRST, FORWARD, FINISH = range(3)
+    own_copy.wait()
+    settle(0)
+    early[0][FIRST]()
+    send_deep(0)
+    settle(1)
+    early[1][FIRST]()
+    send_deep(1)
+    for unit in (0, 1):
+        early[unit][FORWARD]()
+    for unit in (0, 1):
+        early[unit][FINISH]()
+        late[unit][FIRST]()
+    for group in ((2, 3, 4), (5, 6, 7)):
+        for unit in group:
+            wait_deep(*UNITS[unit])
+            early[unit][FIRST]()
+        for unit in group:
+            early[unit][FORWARD]()
+        for unit in group:
+            early[unit][FINISH]()
+            late[unit][FIRST]()
+        if group[0] == 2:
+            for unit in (0, 1):
+                late[unit][FORWARD]()
+    copy(tokens, chip_tokens.at[1], token_sems.at[0], token_sems.at[1], {"core": core}).wait_recv()
+    late[0][FINISH]()
+    project(0)
+    late[1][FINISH]()
+    late[2][FORWARD]()
+    late[4][FORWARD]()
+    late[3][FORWARD]()
+    join(0)
+    expand(0, True, False)
+    for unit in (2, 4, 3):
+        late[unit][FINISH]()
+        project(UNITS[unit][1])
+    late[5][FORWARD]()
+    late[7][FORWARD]()
+    late[6][FORWARD]()
+    for r in (1, 2, 3):
+        join(r)
+    late[5][FINISH]()
+    expand(1, False, False)
+    late[7][FINISH]()
+    expand(2, False, False)
+    late[6][FINISH]()
+    expand(3, False, True)
+    for quarter in range(4):
+        copy(
+            arrived.at[quarter],
+            arrived.at[quarter],
+            swap_send.at[quarter],
+            swap_recv.at[quarter],
+            {"core": core},
+        ).wait_recv()
+        columns = slice(quarter * QUARTER, quarter * QUARTER + QUARTER)
+        value[:, columns] = (total[0, quarter] + arrived[quarter]).astype(jnp.bfloat16)
+    for made in started:
+        made.wait_send()
+
+
 def value_part(tokens, proj_in, proj_out):
-    f32 = jnp.float32
-    places = ("y", "zh", "x")
-    swap = [(0, 1), (1, 0)]
-    other_tokens = lax.ppermute(tokens, "core", swap)
-    in_rows = lax.all_gather(proj_in.T, places, axis=0, tiled=True)
-    out_rows = lax.all_gather(proj_out, places, axis=0, tiled=True)
-    contract = (((1,), (1,)), ((), ()))
-    chip_tokens = jnp.concatenate([tokens, other_tokens], axis=0)
-    partial = lax.dot_general(chip_tokens, in_rows, contract, preferred_element_type=f32)
-    other = lax.ppermute(partial, "ch", swap)
-    low_rank = (partial + other).astype(jnp.bfloat16)
-    sent = jnp.dot(low_rank[ROWS:], out_rows, preferred_element_type=f32)
-    arrived = lax.ppermute(sent, "core", swap)
-    kept = jnp.dot(low_rank[:ROWS], out_rows, preferred_element_type=f32)
-    return (kept + arrived).astype(jnp.bfloat16)
+    f32, bf16 = jnp.float32, jnp.bfloat16
+    pad = ((0, 4), (0, 0))
+    dma = pltpu.SemaphoreType.DMA
+    return pl.pallas_call(
+        value_kernel,
+        out_shape=jax.ShapeDtypeStruct((ROWS, WIDE), bf16),
+        in_specs=[pl.BlockSpec(memory_space=pltpu.VMEM)] * 3,
+        out_specs=pl.BlockSpec(memory_space=pltpu.VMEM),
+        scratch_shapes=[
+            pltpu.VMEM((2, ROWS, WIDE), bf16),
+            pltpu.VMEM((2, 4, 16, QUARTER), bf16),
+            pltpu.VMEM((2, 4, 4, 4, BLOCK, QUARTER), bf16),
+            pltpu.VMEM((4, 2 * ROWS, 4 * BLOCK), f32),
+            pltpu.VMEM((4, 2 * ROWS, 4 * BLOCK), f32),
+            pltpu.VMEM((4, 2 * ROWS, 4 * BLOCK), bf16),
+            pltpu.VMEM((2, 4, ROWS, QUARTER), f32),
+            pltpu.VMEM((4, ROWS, QUARTER), f32),
+            dma,
+            dma((2,)),
+            dma((2, 3)),
+            dma((2, 3)),
+            dma((2, 3)),
+            dma((2, 3)),
+            dma((8, 8)),
+            dma((8, 8)),
+            dma((4,)),
+            dma((4,)),
+            dma((4,)),
+            dma((4,)),
+        ],
+        compiler_params=pltpu.CompilerParams(
+            collective_id=0, has_side_effects=True, vmem_limit_bytes=56 * 2**20
+        ),
+    )(tokens, jnp.pad(proj_in.T, pad), jnp.pad(proj_out, pad))
 
 
 def per_device(

time: 361 us -> 197 us (0.55)
  waiting for transfers between devices: 236 us -> 30.3 us
  Pallas kernels: 16.9 us -> 129 us
  starting transfers between devices: 53 us -> 24.4 us
  local copies, waits for them, and re-layouts: 23.8 us -> 9.69 us
  between operations: 13.6 us -> 0.21 us
  matrix products: 13.3 us -> 0 us
    all_gather x2 -> x0, waiting for transfers between devices: 204 us -> none  [the longest x1 110 us: value_part(): in_rows = lax.all_gather(proj_in.T, places, axis=0, tiled=True)]
    pallas_call x0 -> x1, Pallas kernels: none -> 112 us  [value_part(): pl.pallas_call(value_kernel, out_shape=jax.ShapeDtypeStruct((ROWS, WIDE),...]
    ppermute x3 -> x0, starting transfers between devices: 20.7 us -> none  [the longest x1 8.86 us: value_part(): other = lax.ppermute(partial, 'ch', swap)]
    unnamed x20 -> x22, local copies, waits for them, and re-layouts: 22.7 us -> 3.77 us
    dot_general x3 -> x0, matrix products: 13.3 us -> none  [the longest x1 4.95 us: value_part(): lax.dot_general(chip_tokens, in_rows, contract, preferred_element_type=f32)]
    all_to_all x1, starting transfers between devices: 19.4 us -> 11.4 us  [long_part(): lax.all_to_all(sent, SEQ_AXES, split_axis=0, concat_axis=0, tiled=True)]
  transfers between devices with their start and end apart: 9 -> 4, of which waited for: 6 -> 3; matrix products, arithmetic and copies ran while one was open for 8% -> 4% of each run, Pallas kernels for 0% -> 57%
where the time goes in v1:
time: 197 us; the launch traced here: 196 us
  Pallas kernels  129 us (65%)
  waiting for transfers between devices  30.3 us (15%)
  starting transfers between devices  24.4 us (12%)
  local copies, waits for them, and re-layouts  9.69 us (5%)
  other arithmetic  3.04 us (2%)
    pallas_call x1, Pallas kernels, value_part(): pl.pallas_call(value_kernel, out_shape=jax.ShapeDtypeStruct((ROWS, WIDE),...  112 us
    all_to_all x1, waiting for transfers between devices, long_part(): lax.all_to_all(before, SEQ_AXES, split_axis=0, concat_axis=0, tiled=True)  15 us
    all_to_all x1, waiting for transfers between devices, long_part(): lax.all_to_all(sent, SEQ_AXES, split_axis=0, concat_axis=0, tiled=True)  14.1 us
    all_to_all x1, starting transfers between devices, long_part(): lax.all_to_all(sent, SEQ_AXES, split_axis=0, concat_axis=0, tiled=True)  11.4 us
    pallas_call x1, Pallas kernels, long_part(): pl.pallas_call(out_kernel, out_shape=jax.ShapeDtypeStruct((ROWS, WIDE), j...  7.97 us
    ppermute x2, starting transfers between devices, edge_of(): edge = lax.ppermute(last, SEQ_AXES, ring)  6.53 us
    all_to_all x1, starting transfers between devices, long_part(): lax.all_to_all(before, SEQ_AXES, split_axis=0, concat_axis=0, tiled=True)  6.48 us
    pallas_call x1, Pallas kernels, long_part(): pl.pallas_call(mix_kernel, out_shape=(jax.ShapeDtypeStruct((ROWS, TILES,...  6.48 us
  transfers between devices with their start and end apart: 4, of which 3 were waited for; matrix products, arithmetic and copies ran while one was open for 4% of the time, Pallas kernels for 57%

profile of v1, /device:TPU:1, one launch (start us, length us, event | category | flops | bytes accessed | tf_op | source)
XLA Modules:
  0.0 196.5 jit_solution(6588566233300351414)
XLA Ops:
  0.0 1.0 slice_bitcast_fusion.3
  1.0 0.7 pad_maximum_fusion
  1.7 4.6 %collective-permute-start = (bf16[2,6,4096]{2,1,0:T(8,128)(2,1)}, bf16[2,6,4096]{2,1,0:T(8,128)(2,1)S(1)}, u32[]{:S(2)}, u32[]{:S(2)}) collective-permute-start(bf16[2,6,4096]{2,1,0:T(8,128)(2,1)} %pad_maximum_fusion), channel_id=1, source_target_pairs={{0,2},{2,4},{4,6},{6,8},{8,10},{10,12},{12,14},{14,16},{16,18},{18... | collective-permute-start | bytes 294920 | tf_op jit(solution)/shard_map/ppermute | solution.py:484
  6.3 1.6 pad.21.pad_in
  7.9 1.6 pad.22.pad_out
  9.4 111.9 %shard_map.91.value = bf16[128,4096]{1,0:T(8,128)(2,1)} custom-call(bf16[128,4096]{1,0:T(8,128)(2,1)} %tokens.1, bf16[16,4096]{1,0:T(8,128)(2,1)} %pad.21.pad_in, bf16[16,4096]{1,0:T(8,128)(2,1)} %pad.22.pad_out), custom_call_target="tpu_custom_call" | custom-call | tf_op jit(solution)/shard_map/pallas_call | solution.py:443
  121.4 1.6 slice_bitcast_fusion.2
  123.0 1.9 collective-permute-start.1
  124.9 0.1 multiply_bitcast_fusion
  125.0 0.2 reshape.18.taps
  125.2 0.1 copy.10
  125.3 1.3 collective-permute-done.1
  126.5 0.9 bitcast_convert_fusion.value_edge
  127.5 6.5 %shard_map.92 = (f32[128,32,128]{2,1,0:T(8,128)S(1)}, f32[512,128]{1,0:T(8,128)}) custom-call(bf16[128,4096]{1,0:T(8,128)(2,1)S(1)} %copy-done.3, bf16[128,4096]{1,0:T(8,128)(2,1)S(1)} %copy-done, f32[8,4096]{1,0:T(8,128)S(1)} %get-tuple-element.11.key_edge, f32[8,4096]{1,0:T(8,128)S(1)} %bitcast_convert_fusion.value_edge, ...), custom_call_target="tpu_custom_call" | custom-call | tf_op jit(solution)/shard_map/pallas_call | solution.py:148
  134.0 1.3 copy-done.1
  135.3 11.4 %all-to-all-start = ((f32[128,4,128]{2,1,0:T(4,128)}), f32[128,4,128]{2,1,0:T(4,128)S(1)}, u32[]{:S(2)}, u32[]{:S(2)}) async-start(f32[128,4,128]{2,1,0:T(4,128)} %bitcast.7), calls=%async_computation | async-start | bytes 524288 | tf_op jit(solution)/shard_map/all_to_all | solution.py:159
  146.8 1.4 multiply_exponential_fusion.decay
  148.2 14.1 %all-to-all-done.arrived = f32[128,4,128]{2,1,0:T(4,128)S(1)} async-done(((f32[128,4,128]{2,1,0:T(4,128)}), f32[128,4,128]{2,1,0:T(4,128)S(1)}, u32[]{:S(2)}, u32[]{:S(2)}) %all-to-all-start) | async-done | bytes 262176 | tf_op jit(solution)/shard_map/all_to_all | solution.py:159
  162.2 0.7 copy-done.6
  162.9 2.4 %shard_map.93 = f32[128,4,128]{2,1,0:T(4,128)} custom-call(f32[128,4,128]{2,1,0:T(4,128)} %copy-done.6, f32[4,128]{1,0:T(4,128)} %multiply_exponential_fusion.decay), custom_call_target="tpu_custom_call" | custom-call | tf_op jit(solution)/shard_map/pallas_call | solution.py:162
  165.4 6.5 %all-to-all-start.1 = ((f32[128,4,128]{2,1,0:T(4,128)}), f32[128,4,128]{2,1,0:T(4,128)S(1)}, u32[]{:S(2)}, u32[]{:S(2)}) async-start(f32[128,4,128]{2,1,0:T(4,128)} %shard_map.93), calls=%async_computation.1 | async-start | bytes 524288 | tf_op jit(solution)/shard_map/all_to_all | solution.py:165
  171.9 15.0 %all-to-all-done.1 = f32[128,4,128]{2,1,0:T(4,128)S(1)} async-done(((f32[128,4,128]{2,1,0:T(4,128)}), f32[128,4,128]{2,1,0:T(4,128)S(1)}, u32[]{:S(2)}, u32[]{:S(2)}) %all-to-all-start.1) | async-done | bytes 262176 | tf_op jit(solution)/shard_map/all_to_all | solution.py:165
  186.9 1.6 copy-done.2
  188.5 8.0 %shard_map.94 = bf16[128,4096]{1,0:T(8,128)(2,1)} custom-call(bf16[128,4096]{1,0:T(8,128)(2,1)S(1)} %copy-done.4, f32[8,4096]{1,0:T(8,128)S(1)} %get-tuple-element.12.query_edge, f32[128,32,128]{2,1,0:T(8,128)S(1)} %copy-done.2, f32[512,128]{1,0:T(8,128)S(1)} %bitcast.27, f32[3,7,4,8,128]{4,3,2,1,0:T(8,128)S(1)} %reshape.18.taps, ...), custom_call_target="tpu_custom_call" | custom-call | tf_op jit(solution)/shard_map/pallas_call | solution.py:166
  (21 shorter events, 0.1 us)
Async XLA Ops:
  0.0 124.9 %copy-start.9 = (f32[16,4096]{1,0:T(8,128)S(1)}, f32[16,4096]{1,0:T(8,128)}, u32[]{:S(2)}) copy-start(f32[16,4096]{1,0:T(8,128)} %param.15) | copy-start | bytes 786436
  0.0 124.9 %copy-start.8 = (f32[16,4096]{1,0:T(8,128)S(1)}, f32[16,4096]{1,0:T(8,128)}, u32[]{:S(2)}) copy-start(f32[16,4096]{1,0:T(8,128)} %param.16) | copy-start | bytes 786436
  1.7 123.4 %copy-start.7 = (f32[3,7,4096]{2,1,0:T(8,128)S(1)}, f32[3,7,4096]{2,1,0:T(8,128)}, u32[]{:S(2)}) copy-start(f32[3,7,4096]{2,1,0:T(8,128)} %param.14) | copy-start | bytes 1032196
  1.7 125.7 %collective-permute-start = (bf16[2,6,4096]{2,1,0:T(8,128)(2,1)}, bf16[2,6,4096]{2,1,0:T(8,128)(2,1)S(1)}, u32[]{:S(2)}, u32[]{:S(2)}) collective-permute-start(bf16[2,6,4096]{2,1,0:T(8,128)(2,1)} %pad_maximum_fusion), channel_id=1, source_target_pairs={{0,2},{2,4},{4,6},{6,8},{8,10},{10,12},{12,14},{14,16},{16,18},{18... | collective-permute-start | bytes 294920 | tf_op jit(solution)/shard_map/ppermute | solution.py:484
  121.3 6.1 %copy-start = (bf16[128,4096]{1,0:T(8,128)(2,1)S(1)}, bf16[128,4096]{1,0:T(8,128)(2,1)}, u32[]{:S(2)}) copy-start(bf16[128,4096]{1,0:T(8,128)(2,1)} %shard_map.91.value) | copy-start | bytes 3145732
  121.3 6.1 %copy-start.3 = (bf16[128,4096]{1,0:T(8,128)(2,1)S(1)}, bf16[128,4096]{1,0:T(8,128)(2,1)}, u32[]{:S(2)}) copy-start(bf16[128,4096]{1,0:T(8,128)(2,1)} %key.1) | copy-start | bytes 3145732
  123.0 3.5 %collective-permute-start.1 = (bf16[1,6,4096]{2,1,0:T(8,128)(2,1)}, bf16[1,6,4096]{2,1,0:T(8,128)(2,1)}, u32[]{:S(2)}, u32[]{:S(2)}) collective-permute-start(bf16[1,6,4096]{2,1,0:T(8,128)(2,1)} %slice_bitcast_fusion.2), channel_id=1, source_target_pairs={{0,2},{2,4},{4,6},{6,8},{8,10},{10,12},{12,14},{14,16},{16,18},{18... | collective-permute-start | bytes 147464 | tf_op jit(solution)/shard_map/ppermute | solution.py:484
  127.5 59.4 %copy-start.5 = (f32[4096]{0:T(1024)S(1)}, f32[4096]{0:T(1024)}, u32[]{:S(2)}) copy-start(f32[4096]{0:T(1024)} %param.17) | copy-start | bytes 49156
  134.0 1.3 copy-start.1
  135.3 51.6 %copy-start.4 = (bf16[128,4096]{1,0:T(8,128)(2,1)S(1)}, bf16[128,4096]{1,0:T(8,128)(2,1)}, u32[]{:S(2)}) copy-start(bf16[128,4096]{1,0:T(8,128)(2,1)} %query.1) | copy-start | bytes 3145732
  135.3 26.9 %all-to-all-start = ((f32[128,4,128]{2,1,0:T(4,128)}), f32[128,4,128]{2,1,0:T(4,128)S(1)}, u32[]{:S(2)}, u32[]{:S(2)}) async-start(f32[128,4,128]{2,1,0:T(4,128)} %bitcast.7), calls=%async_computation | async-start | bytes 524288 | tf_op jit(solution)/shard_map/all_to_all | solution.py:159
  162.2 0.7 copy-start.6
  165.4 21.6 %all-to-all-start.1 = ((f32[128,4,128]{2,1,0:T(4,128)}), f32[128,4,128]{2,1,0:T(4,128)S(1)}, u32[]{:S(2)}, u32[]{:S(2)}) async-start(f32[128,4,128]{2,1,0:T(4,128)} %shard_map.93), calls=%async_computation.1 | async-start | bytes 524288 | tf_op jit(solution)/shard_map/all_to_all | solution.py:165
  186.9 1.6 copy-start.2

commit v2 on v1

v2 whole, which is shorter than its diff:
```python
import jax
import jax.numpy as jnp
from jax import lax
from jax.experimental import pallas as pl
from jax.experimental.pallas import tpu as pltpu
from jax.sharding import Mesh
from jax.sharding import PartitionSpec as P

ROWS = 128
WIDE = 4096
LANES = 128
TILES = WIDE // LANES
GROUPS = TILES // 8
MODES = 16
TAPS = 7
SEQ_AXES = ("y", "zh", "x", "core")
MESH = pl.DeviceIdType.MESH
BLOCK = 48
QUARTER = 1024
RANKS = 12
UNITS = ((0, 0), (1, 0), (0, 1), (0, 3), (0, 2), (1, 1), (1, 3), (1, 2))


def lanes_of(tile):
    return slice(tile * LANES, (tile + 1) * LANES)


def spread(source, edge, first_block, scratch):
    for tile in range(TILES):
        above = edge[:, lanes_of(tile)].astype(jnp.float32)
        scratch[tile * 8 : tile * 8 + 8, :] = jnp.where(first_block, 0.0, above)

    @pl.loop(0, ROWS // 16)
    def _(pair):
        for tile in range(TILES):
            rows = pl.ds(pl.multiple_of(pair * 16, 16), 16)
            block = source[rows, lanes_of(tile)].astype(jnp.float32)
            base = pl.multiple_of((2 * pair + 1) * TILES * 8 + tile * 8, 8)
            scratch[pl.ds(base, 8), :] = block[:8]
            scratch[pl.ds(base + TILES * 8, 8), :] = block[8:]


def row_of(scratch, eight, group, row):
    start = (eight + (1 if row >= 0 else 0)) * TILES * 8 + group * 64 + row % 8
    return scratch[pl.ds(start, 8, stride=8), :]


def short(rows, taps, step):
    result = taps[0] * rows[step + 6]
    for offset in range(1, TAPS):
        result = result + taps[offset] * rows[step + 6 - offset]
    return result


def summed(terms):
    while len(terms) > 1:
        terms = [terms[i] + terms[i + 1] for i in range(0, len(terms), 2)]
    return terms[0]


def operator_kernel(
    tokens,
    pad_in,
    pad_out,
    query_in,
    key_in,
    short_taps,
    residues,
    mode_rates,
    skip_gain,
    out,
    value,
    chip_tokens,
    stage,
    weights,
    partial,
    theirs,
    low,
    total,
    arrived,
    edges,
    rows,
    tap_rows,
    rate_rows,
    weight_rows,
    queries,
    mixed,
    local,
    states,
    carried,
    group_states,
    group_before,
    deep_states,
    wide_states,
    own_sem,
    token_sems,
    stage_send,
    stage_recv,
    deep_send,
    deep_recv,
    ring_send,
    ring_recv,
    part_send,
    part_recv,
    swap_send,
    swap_recv,
    edge_send,
    edge_recv,
    near_send,
    near_recv,
    scan_send,
    scan_recv,
    back_send,
    back_recv,
):
    y, zh, x = lax.axis_index("y"), lax.axis_index("zh"), lax.axis_index("x")
    core, ch = lax.axis_index("core"), lax.axis_index("ch")
    place = {"x": x, "y": y, "zh": zh}
    pads = (pad_in, pad_out)
    started = []
    near = x * 2 + core
    block_at = (y * 4 + zh) * 8 + near
    first_block = block_at == 0

    def step(position, by):
        return lax.rem(position + by, 4)

    def copy(source, target, send, recv, device):
        return pltpu.make_async_remote_copy(
            src_ref=source,
            dst_ref=target,
            send_sem=send,
            recv_sem=recv,
            device_id=device,
            device_id_type=MESH,
        )

    def send(*arguments):
        made = copy(*arguments)
        made.start()
        started.append(made)

    def near_device(by):
        to = lax.rem(near + by, 8)
        return to, {"x": to // 2, "core": lax.rem(to, 2)}

    def block_device(by):
        to = lax.rem(block_at + by, 128)
        return {
            "y": to // 32,
            "zh": lax.rem(to // 8, 4),
            "x": lax.rem(to // 2, 4),
            "core": lax.rem(to, 2),
        }

    def send_edge(i, source):
        send(
            source.at[pl.ds(ROWS - 8, 8)],
            edges.at[i],
            edge_send.at[i],
            edge_recv.at[i],
            block_device(1),
        )

    def wait_edge(i):
        edge = edges.at[i]
        copy(edge, edge, edge_send.at[i], edge_recv.at[i], {"ch": ch}).wait_recv()

    barrier = pltpu.get_barrier_semaphore()
    greeted = [{"ch": 1 - ch}, block_device(1), block_device(127)]
    greeted += [near_device(by)[1] for by in range(1, 8)]
    greeted += [{axis: step(place[axis], by)} for axis in ("zh", "y") for by in (1, 2, 3)]
    for device in greeted:
        pl.semaphore_signal(barrier, inc=1, device_id=device, device_id_type=MESH)
    own_copy = pltpu.make_async_copy(tokens, chip_tokens.at[0], own_sem)
    own_copy.start()
    pl.semaphore_wait(barrier, len(greeted))

    for f in range(2):
        for by in (1, 3, 2):
            to = step(x, by)
            columns = pl.ds(pl.multiple_of(to * QUARTER, QUARTER), QUARTER)
            send(
                pads[f].at[:, columns],
                stage.at[f, x],
                stage_send.at[f, by - 1],
                stage_recv.at[f, by - 1],
                {"x": to},
            )
    send(tokens, chip_tokens.at[1], token_sems.at[0], token_sems.at[1], {"core": 1 - core})
    for i, source in enumerate((query_in, key_in)):
        send_edge(i, source)

    def settle(f):
        columns = pl.ds(pl.multiple_of(x * QUARTER, QUARTER), QUARTER)
        own = pltpu.make_async_copy(pads[f].at[:, columns], stage.at[f, x], own_sem)
        own.start()
        own.wait()
        for by in (1, 3, 2):
            came = stage.at[f, step(x, 4 - by)]
            copy(came, came, stage_send.at[f, by - 1], stage_recv.at[f, by - 1], {"x": x}).wait_recv()
        parts = [stage[f, i].astype(jnp.float32) for i in range(4)]
        weights[f, y, zh, x] = jnp.concatenate(parts, axis=0).astype(jnp.bfloat16)

    def send_deep(f):
        block = weights.at[f, y, zh, x]
        for by in (1, 3, 2):
            send(block, block, deep_send.at[f, by - 1], deep_recv.at[f, by - 1], {"zh": step(zh, by)})

    def wait_deep(f, r):
        by = 4 - r
        block = weights.at[f, y, step(zh, r), x]
        copy(block, block, deep_send.at[f, by - 1], deep_recv.at[f, by - 1], {"zh": zh}).wait_recv()

    def ring(unit, late):
        f, r = UNITS[unit]
        deep = step(zh, r)
        across = (f + r) % 2 == 0
        axis = "x" if across != late else "y"
        at = place[axis]

        def item(i, half=None):
            if not late:
                columns = slice(None) if half is None else slice(half * 512, half * 512 + 512)
                if across:
                    return weights.at[f, y, deep, i, :, columns]
                return weights.at[f, i, deep, x, :, columns]
            blocks = slice(None) if half is None else slice(half * 2, half * 2 + 2)
            if across:
                return weights.at[f, i, deep, blocks]
            return weights.at[f, blocks, deep, i]

        base = 4 if late else 0
        plus, minus = step(at, 1), step(at, 3)

        def out(ref, slot, to):
            send(ref, ref, ring_send.at[unit, base + slot], ring_recv.at[unit, base + slot], {axis: to})

        def landed(ref, slot):
            copy(
                ref, ref, ring_send.at[unit, base + slot], ring_recv.at[unit, base + slot], {axis: at}
            ).wait_recv()

        def first():
            out(item(at), 0, plus)
            out(item(at), 1, minus)

        def forward():
            landed(item(minus), 0)
            out(item(minus, 0), 2, plus)
            landed(item(plus), 1)
            out(item(plus, 1), 3, minus)

        def finish():
            landed(item(step(at, 2), 0), 2)
            landed(item(step(at, 2), 1), 3)

        return first, forward, finish

    early = [ring(unit, False) for unit in range(8)]
    late = [ring(unit, True) for unit in range(8)]

    def unit_weights(f, r, quarter):
        return weights[f, :, step(zh, r), quarter].reshape(4 * BLOCK, QUARTER)

    def project(r):
        @pl.loop(0, 4)
        def _(quarter):
            columns = pl.ds(pl.multiple_of(quarter * QUARTER, QUARTER), QUARTER)
            part = lax.dot_general(
                chip_tokens[:, :, columns].reshape(2 * ROWS, QUARTER),
                unit_weights(0, r, quarter),
                (((1,), (1,)), ((), ())),
                preferred_element_type=jnp.float32,
            )

            @pl.when(quarter == 0)
            def _():
                partial[r] = part

            @pl.when(quarter > 0)
            def _():
                partial[r] += part

        send(partial.at[r], theirs.at[r], part_send.at[r], part_recv.at[r], {"ch": 1 - ch})

    def join(r):
        copy(partial.at[r], theirs.at[r], part_send.at[r], part_recv.at[r], {"ch": ch}).wait_recv()
        low[r] = (partial[r] + theirs[r]).astype(jnp.bfloat16)

    def expand(r, opening, closing):
        for quarter in range(4):
            part = jnp.dot(
                low[r], unit_weights(1, r, quarter), preferred_element_type=jnp.float32
            ).reshape(2, ROWS, QUARTER)
            if opening:
                total[:, quarter] = part
            else:
                total[:, quarter] += part
            if closing:
                send(
                    total.at[1, quarter],
                    arrived.at[quarter],
                    swap_send.at[quarter],
                    swap_recv.at[quarter],
                    {"core": 1 - core},
                )


    def tap_of(branch, offset, group):
        start = (branch * TILES + group * 8) * 8 + offset
        return tap_rows[pl.ds(start, 8, stride=8), :]

    def mode_of(ref, n, group):
        half, row = n // 8, n % 8
        return ref[half, pl.ds(group * 64 + row, 8, stride=8), :]

    def at_group(group):
        return slice(group * 8, group * 8 + 8)

    def filtered(branch, target):
        for group in range(GROUPS):
            taps = [tap_of(branch, j, group) for j in range(TAPS)]

            @pl.loop(0, ROWS // 8)
            def _(eight):
                window = [row_of(rows, eight, group, r) for r in range(-6, 8)]
                for i in range(8):
                    target(eight * 8 + i, group, short(window, taps, i))

    def prepare():
        for tile in range(TILES):
            for branch in range(3):
                base = (branch * TILES + tile) * 8
                tap_rows[base : base + TAPS, :] = short_taps[branch, :, lanes_of(tile)]
            for half in range(2):
                modes = slice(half * 8, half * 8 + 8)
                rate = mode_rates[modes, lanes_of(tile)]
                rate_rows[half, tile * 8 : tile * 8 + 8, :] = rate
                weight_rows[half, tile * 8 : tile * 8 + 8, :] = (
                    residues[modes, lanes_of(tile)] * jnp.sqrt(rate)
                )

        def keep_query(t, group, result):
            queries[t, at_group(group), :] = result

        def keep_key(t, group, result):
            mixed[t, at_group(group), :] = result

        wait_edge(0)
        spread(query_in, edges.at[0], first_block, rows)
        filtered(0, keep_query)
        wait_edge(1)
        spread(key_in, edges.at[1], first_block, rows)
        filtered(1, keep_key)

    def mix():
        def keep(t, group, result):
            product = mixed[t, at_group(group), :] * result
            mixed[t, at_group(group), :] = product.astype(jnp.bfloat16).astype(jnp.float32)

        wait_edge(2)
        spread(value, edges.at[2], first_block, rows)
        filtered(2, keep)

    def decays(group):
        return [jnp.exp(-mode_of(rate_rows, n, group)) for n in range(MODES)]

    zeros = (jnp.zeros((8, LANES), jnp.float32),) * MODES

    def summarize(group):
        rates = decays(group)

        def advance(eight, held):
            for i in range(8):
                entry = mixed[eight * 8 + i, at_group(group), :]
                held = tuple(rates[n] * held[n] + entry for n in range(MODES))
            return held

        held = lax.fori_loop(0, ROWS // 8, advance, zeros)
        for n in range(MODES):
            states[n // 8, pl.ds(group * 64 + n % 8, 8, stride=8), :] = held[n]

    def localize(group):
        rates = decays(group)
        weighting = [mode_of(weight_rows, n, group) for n in range(MODES)]

        def advance(eight, held):
            for i in range(8):
                entry = mixed[eight * 8 + i, at_group(group), :]
                held = tuple(rates[n] * held[n] + entry for n in range(MODES))
                local[eight * 8 + i, at_group(group), :] = summed(
                    [weighting[n] * held[n] for n in range(MODES)]
                )
            return held

        lax.fori_loop(0, ROWS // 8, advance, zeros)

    def finish_group(group):
        rates = decays(group)
        skip = skip_gain[at_group(group), :]
        first = tuple(
            mode_of(weight_rows, n, group) * mode_of(carried, n, group) for n in range(MODES)
        )

        def advance(eight, held):
            for i in range(8):
                held = tuple(rates[n] * held[n] for n in range(MODES))
                t = eight * 8 + i
                convolved = local[t, at_group(group), :] + summed(list(held))
                convolved = convolved.astype(jnp.bfloat16).astype(jnp.float32)
                result = queries[t, at_group(group), :] * (
                    convolved + skip * mixed[t, at_group(group), :]
                )
                rows[pl.ds(eight * TILES * 8 + group * 64 + i, 8, stride=8), :] = result
            return held

        lax.fori_loop(0, ROWS // 8, advance, first)

    def near_part(at):
        return pl.ds(pl.multiple_of(at * 32, 32), 32)

    def exchange_states():
        for by in range(1, 8):
            to, device = near_device(by)
            send(
                states.at[:, near_part(to)],
                group_states.at[near],
                near_send.at[by - 1],
                near_recv.at[by - 1],
                device,
            )
        localize(0)
        localize(1)
        rate = rate_rows[:, near_part(near), :]
        one = jnp.exp(-float(ROWS) * rate)
        eight = jnp.exp(-8.0 * ROWS * rate)
        group_states[near] = states[:, near_part(near), :]
        for by in range(1, 8):
            came = group_states.at[lax.rem(near + 8 - by, 8)]
            copy(came, came, near_send.at[by - 1], near_recv.at[by - 1], {"ch": ch}).wait_recv()
        held = jnp.zeros(rate.shape, jnp.float32)
        for k in range(8):
            group_before[k] = held
            held = one * held + group_states[k]

        def across(buffer, axis, slot, own, decay, cover):
            at = place[axis]
            buffer[at] = own
            for by in (1, 3, 2):
                send(
                    buffer.at[at],
                    buffer.at[at],
                    scan_send.at[slot, by - 1],
                    scan_recv.at[slot, by - 1],
                    {axis: step(at, by)},
                )
            cover()
            for by in (1, 3, 2):
                came = buffer.at[step(at, 4 - by)]
                copy(
                    came, came, scan_send.at[slot, by - 1], scan_recv.at[slot, by - 1], {"ch": ch}
                ).wait_recv()
            running = jnp.zeros(own.shape, jnp.float32)
            before = running
            for k in range(4):
                before = jnp.where(at == k, running, before)
                running = decay * running + buffer[k]
            return before, running

        deep_before, deep_total = across(
            deep_states, "zh", 0, held, eight, lambda: (localize(2), localize(3))
        )
        wide_before, _ = across(
            wide_states, "y", 1, deep_total, jnp.exp(-32.0 * ROWS * rate), lambda: None
        )
        shift = jnp.exp(rate * (-8.0 * ROWS * zh.astype(jnp.float32)))
        entering = deep_before + shift * wide_before
        for k in range(8):
            group_before[k] += entering
            entering = one * entering
        for by in range(1, 8):
            to, device = near_device(by)
            send(
                group_before.at[to],
                carried.at[:, near_part(near)],
                back_send.at[by - 1],
                back_recv.at[by - 1],
                device,
            )
        carried[:, near_part(near), :] = group_before[near]
        for by in range(1, 8):
            came = carried.at[:, near_part(lax.rem(near + 8 - by, 8))]
            copy(came, came, back_send.at[by - 1], back_recv.at[by - 1], {"ch": ch}).wait_recv()

    FIRST, FORWARD, FINISH = range(3)
    own_copy.wait()
    settle(0)
    early[0][FIRST]()
    send_deep(0)
    settle(1)
    early[1][FIRST]()
    send_deep(1)
    for unit in (0, 1):
        early[unit][FORWARD]()
    for unit in (0, 1):
        early[unit][FINISH]()
        late[unit][FIRST]()
    for group in ((2, 3, 4), (5, 6, 7)):
        for unit in group:
            wait_deep(*UNITS[unit])
            early[unit][FIRST]()
        for unit in group:
            early[unit][FORWARD]()
        for unit in group:
            early[unit][FINISH]()
            late[unit][FIRST]()
        if group[0] == 2:
            for unit in (0, 1):
                late[unit][FORWARD]()
    prepare()
    copy(tokens, chip_tokens.at[1], token_sems.at[0], token_sems.at[1], {"core": core}).wait_recv()
    late[0][FINISH]()
    project(0)
    late[1][FINISH]()
    late[2][FORWARD]()
    late[4][FORWARD]()
    late[3][FORWARD]()
    join(0)
    expand(0, True, False)
    for unit in (2, 4, 3):
        late[unit][FINISH]()
        project(UNITS[unit][1])
    late[5][FORWARD]()
    late[7][FORWARD]()
    late[6][FORWARD]()
    for r in (1, 2, 3):
        join(r)
    late[5][FINISH]()
    expand(1, False, False)
    late[7][FINISH]()
    expand(2, False, False)
    late[6][FINISH]()
    expand(3, False, True)
    for quarter in range(4):
        copy(
            arrived.at[quarter],
            arrived.at[quarter],
            swap_send.at[quarter],
            swap_recv.at[quarter],
            {"core": core},
        ).wait_recv()
        columns = slice(quarter * QUARTER, quarter * QUARTER + QUARTER)
        value[:, columns] = (total[0, quarter] + arrived[quarter]).astype(jnp.bfloat16)
    send_edge(2, value)
    mix()
    for group in range(GROUPS):
        summarize(group)
    exchange_states()
    for group in range(GROUPS):
        finish_group(group)

    @pl.loop(0, ROWS // 16)
    def _(pair):
        for tile in range(TILES):
            base = pl.multiple_of(2 * pair * TILES * 8 + tile * 8, 8)
            block = jnp.concatenate(
                [rows[pl.ds(base, 8), :], rows[pl.ds(base + TILES * 8, 8), :]], axis=0
            )
            out[pl.ds(pl.multiple_of(pair * 16, 16), 16), lanes_of(tile)] = block.astype(
                jnp.bfloat16
            )

    for made in started:
        made.wait_send()


def per_device(
    tokens, query_in, key_in, proj_in, proj_out, short_taps, residues, mode_rates, skip_gain
):
    f32, bf16 = jnp.float32, jnp.bfloat16
    dma = pltpu.SemaphoreType.DMA
    return pl.pallas_call(
        operator_kernel,
        out_shape=jax.ShapeDtypeStruct((ROWS, WIDE), bf16),
        in_specs=[pl.BlockSpec(memory_space=pltpu.VMEM)] * 9,
        out_specs=pl.BlockSpec(memory_space=pltpu.VMEM),
        scratch_shapes=[
            pltpu.VMEM((ROWS, WIDE), bf16),
            pltpu.VMEM((2, ROWS, WIDE), bf16),
            pltpu.VMEM((2, 4, RANKS, QUARTER), bf16),
            pltpu.VMEM((2, 4, 4, 4, BLOCK, QUARTER), bf16),
            pltpu.VMEM((4, 2 * ROWS, 4 * BLOCK), f32),
            pltpu.VMEM((4, 2 * ROWS, 4 * BLOCK), f32),
            pltpu.VMEM((4, 2 * ROWS, 4 * BLOCK), bf16),
            pltpu.VMEM((2, 4, ROWS, QUARTER), f32),
            pltpu.VMEM((4, ROWS, QUARTER), f32),
            pltpu.VMEM((3, 8, WIDE), bf16),
            pltpu.VMEM(((ROWS + 8) * TILES, LANES), f32),
            pltpu.VMEM((3 * TILES * 8, LANES), f32),
            pltpu.VMEM((2, TILES * 8, LANES), f32),
            pltpu.VMEM((2, TILES * 8, LANES), f32),
            pltpu.VMEM((ROWS, TILES, LANES), f32),
            pltpu.VMEM((ROWS, TILES, LANES), f32),
            pltpu.VMEM((ROWS, TILES, LANES), f32),
            pltpu.VMEM((2, TILES * 8, LANES), f32),
            pltpu.VMEM((2, TILES * 8, LANES), f32),
            pltpu.VMEM((8, 2, 32, LANES), f32),
            pltpu.VMEM((8, 2, 32, LANES), f32),
            pltpu.VMEM((4, 2, 32, LANES), f32),
            pltpu.VMEM((4, 2, 32, LANES), f32),
            dma,
            dma((2,)),
            dma((2, 3)),
            dma((2, 3)),
            dma((2, 3)),
            dma((2, 3)),
            dma((8, 8)),
            dma((8, 8)),
            dma((4,)),
            dma((4,)),
            dma((4,)),
            dma((4,)),
            dma((3,)),
            dma((3,)),
            dma((7,)),
            dma((7,)),
            dma((2, 3)),
            dma((2, 3)),
            dma((7,)),
            dma((7,)),
        ],
        compiler_params=pltpu.CompilerParams(
            collective_id=0, has_side_effects=True, vmem_limit_bytes=60 * 2**20
        ),
    )(
        tokens,
        proj_in.T,
        proj_out,
        query_in,
        key_in,
        short_taps,
        residues,
        mode_rates,
        skip_gain.reshape(TILES, LANES),
    )


def solution(mesh):
    split = Mesh(mesh.devices.reshape(4, 4, 4, 2, 2), ("y", "zh", "x", "core", "ch"))
    both = P(SEQ_AXES, "ch")
    placed = (
        both,
        both,
        both,
        P("ch", SEQ_AXES),
        both,
        P(None, None, "ch"),
        P(None, "ch"),
        P(None, "ch"),
        P("ch"),
    )
    return jax.shard_map(
        per_device, mesh=split, in_specs=placed, out_specs=both, check_vma=False
    )
```

time: 197 us -> 145 us (0.74)
  waiting for transfers between devices: 30.3 us -> 0 us
  starting transfers between devices: 24.4 us -> 0 us
  Pallas kernels: 129 us -> 143 us
  local copies, waits for them, and re-layouts: 9.69 us -> 2.29 us
  other arithmetic: 3.04 us -> 0 us
    all_to_all x2 -> x0, waiting for transfers between devices: 29.1 us -> none  [the longest x1 15 us: long_part(): lax.all_to_all(before, SEQ_AXES, split_axis=0, concat_axis=0, tiled=True)]
    all_to_all x2 -> x0, starting transfers between devices: 17.9 us -> none  [the longest x1 11.4 us: long_part(): lax.all_to_all(sent, SEQ_AXES, split_axis=0, concat_axis=0, tiled=True)]
    pallas_call x4 -> x1, Pallas kernels: 129 us -> 143 us  [per_device(): pl.pallas_call(operator_kernel, out_shape=jax.ShapeDtypeStruct((ROWS, WID...]
    ppermute x2 -> x0, starting transfers between devices: 6.53 us -> none  [edge_of(): edge = lax.ppermute(last, SEQ_AXES, ring)]
    pad x2 -> x0, local copies, waits for them, and re-layouts: 3.14 us -> none  [the longest x1 1.58 us: value_part(): jnp.pad(proj_in.T, pad)]
  transfers between devices with their start and end apart: 4 -> 0, of which waited for: 3 -> 0; matrix products, arithmetic and copies ran while one was open for 4% -> 0% of each run, Pallas kernels for 57% -> 0%
where the time goes in v2:
time: 145 us
  Pallas kernels  143 us (99%)
  local copies, waits for them, and re-layouts  2.29 us (2%)
    pallas_call x1, Pallas kernels, per_device(): pl.pallas_call(operator_kernel, out_shape=jax.ShapeDtypeStruct((ROWS, WID...  143 us

profile of v2, /device:TPU:1, one launch (start us, length us, event | category | flops | bytes accessed | tf_op | source)
XLA Modules:
  0.0 144.8 jit_solution(11229151798399820146)
XLA Ops:
  0.0 142.5 %shard_map.91 = bf16[128,4096]{1,0:T(8,128)(2,1)} custom-call(bf16[128,4096]{1,0:T(8,128)(2,1)} %tokens.1, bf16[12,4096]{1,0:T(8,128)(2,1)} %bitcast.2, bf16[12,4096]{1,0:T(8,128)(2,1)} %pad_out.1, bf16[128,4096]{1,0:T(8,128)(2,1)} %query_in.1, bf16[128,4096]{1,0:T(8,128)(2,1)} %key_in.1, f32[3,7,4096]{2,1,0:T(8,128)} %short_taps.1, f32[16,4096]{1,0:T(8,128)} %residues.1, ...), custom_call_target="tpu_custom_call" | custom-call | tf_op jit(solution)/shard_map/pallas_call | solution.py:583
  142.5 2.3 %copy.11 = bf16[128,4096]{1,0:T(8,128)(2,1)} copy(bf16[128,4096]{1,0:T(8,128)(2,1)} %shard_map.91) | data formatting | bytes 2097152

commit v3 on v2

--- a/solution.py
+++ b/solution.py
@@ -25,10 +25,14 @@
     return slice(tile * LANES, (tile + 1) * LANES)
 
 
-def spread(source, edge, first_block, scratch):
+def spread_edge(edge, first_block, scratch):
     for tile in range(TILES):
         above = edge[:, lanes_of(tile)].astype(jnp.float32)
         scratch[tile * 8 : tile * 8 + 8, :] = jnp.where(first_block, 0.0, above)
+
+
+def spread(source, edge, first_block, scratch):
+    spread_edge(edge, first_block, scratch)
 
     @pl.loop(0, ROWS // 16)
     def _(pair):
@@ -69,7 +73,7 @@
     mode_rates,
     skip_gain,
     out,
-    value,
+    last,
     chip_tokens,
     stage,
     weights,
@@ -202,44 +206,15 @@
         parts = [stage[f, i].astype(jnp.float32) for i in range(4)]
         weights[f, y, zh, x] = jnp.concatenate(parts, axis=0).astype(jnp.bfloat16)
 
-    def send_deep(f):
-        block = weights.at[f, y, zh, x]
-        for by in (1, 3, 2):
-            send(block, block, deep_send.at[f, by - 1], deep_recv.at[f, by - 1], {"zh": step(zh, by)})
-
-    def wait_deep(f, r):
-        by = 4 - r
-        block = weights.at[f, y, step(zh, r), x]
-        copy(block, block, deep_send.at[f, by - 1], deep_recv.at[f, by - 1], {"zh": zh}).wait_recv()
-
-    def ring(unit, late):
-        f, r = UNITS[unit]
-        deep = step(zh, r)
-        across = (f + r) % 2 == 0
-        axis = "x" if across != late else "y"
+    def ring(axis, item, send_sems, recv_sems):
         at = place[axis]
-
-        def item(i, half=None):
-            if not late:
-                columns = slice(None) if half is None else slice(half * 512, half * 512 + 512)
-                if across:
-                    return weights.at[f, y, deep, i, :, columns]
-                return weights.at[f, i, deep, x, :, columns]
-            blocks = slice(None) if half is None else slice(half * 2, half * 2 + 2)
-            if across:
-                return weights.at[f, i, deep, blocks]
-            return weights.at[f, blocks, deep, i]
-
-        base = 4 if late else 0
-        plus, minus = step(at, 1), step(at, 3)
+        plus, minus, far = step(at, 1), step(at, 3), step(at, 2)
 
         def out(ref, slot, to):
-            send(ref, ref, ring_send.at[unit, base + slot], ring_recv.at[unit, base + slot], {axis: to})
+            send(ref, ref, send_sems(slot), recv_sems(slot), {axis: to})
 
         def landed(ref, slot):
-            copy(
-                ref, ref, ring_send.at[unit, base + slot], ring_recv.at[unit, base + slot], {axis: at}
-            ).wait_recv()
+            copy(ref, ref, send_sems(slot), recv_sems(slot), {axis: at}).wait_recv()
 
         def first():
             out(item(at), 0, plus)
@@ -252,13 +227,50 @@
             out(item(plus, 1), 3, minus)
 
         def finish():
-            landed(item(step(at, 2), 0), 2)
-            landed(item(step(at, 2), 1), 3)
+            landed(item(far, 0), 2)
+            landed(item(far, 1), 3)
 
         return first, forward, finish
 
-    early = [ring(unit, False) for unit in range(8)]
-    late = [ring(unit, True) for unit in range(8)]
+    def half_columns(half):
+        return slice(None) if half is None else slice(half * 512, half * 512 + 512)
+
+    def half_blocks(half):
+        return slice(None) if half is None else slice(half * 2, half * 2 + 2)
+
+    def deep_ring(f):
+        return ring(
+            "zh",
+            lambda i, half=None: weights.at[f, y, i, x, :, half_columns(half)],
+            lambda slot: deep_send.at[f, slot],
+            lambda slot: deep_recv.at[f, slot],
+        )
+
+    def unit_ring(unit, late):
+        f, r = UNITS[unit]
+        deep = step(zh, r)
+        across = unit % 2 == 0
+
+        def item(i, half=None):
+            if late:
+                if across:
+                    return weights.at[f, i, deep, half_blocks(half)]
+                return weights.at[f, half_blocks(half), deep, i]
+            if across:
+                return weights.at[f, y, deep, i, :, half_columns(half)]
+            return weights.at[f, i, deep, x, :, half_columns(half)]
+
+        base = 4 if late else 0
+        return ring(
+            "x" if across != late else "y",
+            item,
+            lambda slot: ring_send.at[unit, base + slot],
+            lambda slot: ring_recv.at[unit, base + slot],
+        )
+
+    deep = [deep_ring(f) for f in range(2)]
+    early = [unit_ring(unit, False) for unit in range(8)]
+    late = [unit_ring(unit, True) for unit in range(8)]
 
     def unit_weights(f, r, quarter):
         return weights[f, :, step(zh, r), quarter].reshape(4 * BLOCK, QUARTER)
@@ -318,11 +330,11 @@
     def at_group(group):
         return slice(group * 8, group * 8 + 8)
 
-    def filtered(branch, target):
+    def filtered(branch, target, begin=0, end=ROWS // 8):
         for group in range(GROUPS):
             taps = [tap_of(branch, j, group) for j in range(TAPS)]
 
-            @pl.loop(0, ROWS // 8)
+            @pl.loop(begin, end)
             def _(eight):
                 window = [row_of(rows, eight, group, r) for r in range(-6, 8)]
                 for i in range(8):
@@ -354,32 +366,71 @@
         spread(key_in, edges.at[1], first_block, rows)
         filtered(1, keep_key)
 
+    def gather_value():
+        for quarter in range(4):
+            came = arrived.at[quarter]
+            copy(came, came, swap_send.at[quarter], swap_recv.at[quarter], {"ch": ch}).wait_recv()
+
+        def block_rows(pair):
+            for tile in range(TILES):
+                quarter, columns = tile // 8, lanes_of(tile % 8)
+                where = pl.ds(pl.multiple_of(pair * 16, 16), 16)
+                block = total[0, quarter, where, columns] + arrived[quarter, where, columns]
+                block = block.astype(jnp.bfloat16)
+                if isinstance(pair, int):
+                    last[:, lanes_of(tile)] = block[8:]
+                block = block.astype(jnp.float32)
+                base = pl.multiple_of((2 * pair + 1) * TILES * 8 + tile * 8, 8)
+                rows[pl.ds(base, 8), :] = block[:8]
+                rows[pl.ds(base + TILES * 8, 8), :] = block[8:]
+
+        block_rows(ROWS // 16 - 1)
+        send(last, edges.at[2], edge_send.at[2], edge_recv.at[2], block_device(1))
+        pl.loop(0, ROWS // 16 - 1)(block_rows)
+
     def mix():
         def keep(t, group, result):
             product = mixed[t, at_group(group), :] * result
             mixed[t, at_group(group), :] = product.astype(jnp.bfloat16).astype(jnp.float32)
 
+        filtered(2, keep, 1, ROWS // 8)
+
+    def mix_first():
+        def keep(t, group, result):
+            product = mixed[t, at_group(group), :] * result
+            mixed[t, at_group(group), :] = product.astype(jnp.bfloat16).astype(jnp.float32)
+
         wait_edge(2)
-        spread(value, edges.at[2], first_block, rows)
-        filtered(2, keep)
+        spread_edge(edges.at[2], first_block, rows)
+        filtered(2, keep, 0, 1)
 
     def decays(group):
         return [jnp.exp(-mode_of(rate_rows, n, group)) for n in range(MODES)]
 
     zeros = (jnp.zeros((8, LANES), jnp.float32),) * MODES
 
-    def summarize(group):
-        rates = decays(group)
-
+    def run_modes(group, rates, begin, end, held):
         def advance(eight, held):
             for i in range(8):
                 entry = mixed[eight * 8 + i, at_group(group), :]
                 held = tuple(rates[n] * held[n] + entry for n in range(MODES))
             return held
 
-        held = lax.fori_loop(0, ROWS // 8, advance, zeros)
+        return lax.fori_loop(begin, end, advance, held)
+
+    def store_states(group, held):
         for n in range(MODES):
             states[n // 8, pl.ds(group * 64 + n % 8, 8, stride=8), :] = held[n]
+
+    def summarize(group):
+        store_states(group, run_modes(group, decays(group), 1, ROWS // 8, zeros))
+
+    def summarize_first(group):
+        held = run_modes(group, decays(group), 0, 1, zeros)
+        rest = [jnp.exp(-float(ROWS - 8) * mode_of(rate_rows, n, group)) for n in range(MODES)]
+        store_states(
+            group, [mode_of(states, n, group) + rest[n] * held[n] for n in range(MODES)]
+        )
 
     def localize(group):
         rates = decays(group)
@@ -412,7 +463,7 @@
                 result = queries[t, at_group(group), :] * (
                     convolved + skip * mixed[t, at_group(group), :]
                 )
-                rows[pl.ds(eight * TILES * 8 + group * 64 + i, 8, stride=8), :] = result
+                out[pl.ds(eight * TILES * 8 + group * 64 + i, 8, stride=8), :] = result
             return held
 
         lax.fori_loop(0, ROWS // 8, advance, first)
@@ -494,83 +545,70 @@
             copy(came, came, back_send.at[by - 1], back_recv.at[by - 1], {"ch": ch}).wait_recv()
 
     FIRST, FORWARD, FINISH = range(3)
+
+    def both(rings, pair, action):
+        for unit in (2 * pair, 2 * pair + 1):
+            rings[unit][action]()
+
     own_copy.wait()
     settle(0)
     early[0][FIRST]()
-    send_deep(0)
+    deep[0][FIRST]()
     settle(1)
     early[1][FIRST]()
-    send_deep(1)
-    for unit in (0, 1):
-        early[unit][FORWARD]()
-    for unit in (0, 1):
-        early[unit][FINISH]()
-        late[unit][FIRST]()
-    for group in ((2, 3, 4), (5, 6, 7)):
-        for unit in group:
-            wait_deep(*UNITS[unit])
-            early[unit][FIRST]()
-        for unit in group:
-            early[unit][FORWARD]()
-        for unit in group:
-            early[unit][FINISH]()
-            late[unit][FIRST]()
-        if group[0] == 2:
-            for unit in (0, 1):
-                late[unit][FORWARD]()
+    deep[1][FIRST]()
+    both(early, 0, FORWARD)
+    deep[0][FORWARD]()
+    both(early, 1, FIRST)
+    both(early, 0, FINISH)
+    both(late, 0, FIRST)
+    both(early, 1, FORWARD)
+    deep[0][FINISH]()
+    deep[1][FORWARD]()
+    both(early, 2, FIRST)
+    deep[1][FINISH]()
     prepare()
+    both(late, 0, FORWARD)
+    both(early, 1, FINISH)
+    both(late, 1, FIRST)
+    both(early, 2, FORWARD)
+    both(early, 3, FIRST)
     copy(tokens, chip_tokens.at[1], token_sems.at[0], token_sems.at[1], {"core": core}).wait_recv()
-    late[0][FINISH]()
+    both(late, 0, FINISH)
     project(0)
-    late[1][FINISH]()
-    late[2][FORWARD]()
-    late[4][FORWARD]()
-    late[3][FORWARD]()
+    both(late, 1, FORWARD)
+    both(early, 2, FINISH)
+    both(late, 2, FIRST)
+    both(early, 3, FORWARD)
+    both(late, 1, FINISH)
+    project(1)
+    project(3)
     join(0)
     expand(0, True, False)
-    for unit in (2, 4, 3):
-        late[unit][FINISH]()
-        project(UNITS[unit][1])
-    late[5][FORWARD]()
-    late[7][FORWARD]()
-    late[6][FORWARD]()
-    for r in (1, 2, 3):
-        join(r)
-    late[5][FINISH]()
+    both(late, 2, FORWARD)
+    both(early, 3, FINISH)
+    both(late, 3, FIRST)
+    both(late, 2, FINISH)
+    project(2)
+    join(1)
     expand(1, False, False)
+    join(3)
+    both(late, 3, FORWARD)
+    join(2)
+    late[6][FINISH]()
+    expand(3, False, False)
     late[7][FINISH]()
-    expand(2, False, False)
-    late[6][FINISH]()
-    expand(3, False, True)
-    for quarter in range(4):
-        copy(
-            arrived.at[quarter],
-            arrived.at[quarter],
-            swap_send.at[quarter],
-            swap_recv.at[quarter],
-            {"core": core},
-        ).wait_recv()
-        columns = slice(quarter * QUARTER, quarter * QUARTER + QUARTER)
-        value[:, columns] = (total[0, quarter] + arrived[quarter]).astype(jnp.bfloat16)
-    send_edge(2, value)
+    expand(2, False, True)
+    gather_value()
     mix()
     for group in range(GROUPS):
         summarize(group)
+    mix_first()
+    for group in range(GROUPS):
+        summarize_first(group)
     exchange_states()
     for group in range(GROUPS):
         finish_group(group)
-
-    @pl.loop(0, ROWS // 16)
-    def _(pair):
-        for tile in range(TILES):
-            base = pl.multiple_of(2 * pair * TILES * 8 + tile * 8, 8)
-            block = jnp.concatenate(
-                [rows[pl.ds(base, 8), :], rows[pl.ds(base + TILES * 8, 8), :]], axis=0
-            )
-            out[pl.ds(pl.multiple_of(pair * 16, 16), 16), lanes_of(tile)] = block.astype(
-                jnp.bfloat16
-            )
-
     for made in started:
         made.wait_send()
 
@@ -580,13 +618,13 @@
 ):
     f32, bf16 = jnp.float32, jnp.bfloat16
     dma = pltpu.SemaphoreType.DMA
-    return pl.pallas_call(
+    tiles = pl.pallas_call(
         operator_kernel,
-        out_shape=jax.ShapeDtypeStruct((ROWS, WIDE), bf16),
+        out_shape=jax.ShapeDtypeStruct((ROWS * TILES, LANES), f32),
         in_specs=[pl.BlockSpec(memory_space=pltpu.VMEM)] * 9,
         out_specs=pl.BlockSpec(memory_space=pltpu.VMEM),
         scratch_shapes=[
-            pltpu.VMEM((ROWS, WIDE), bf16),
+            pltpu.VMEM((8, WIDE), bf16),
             pltpu.VMEM((2, ROWS, WIDE), bf16),
             pltpu.VMEM((2, 4, RANKS, QUARTER), bf16),
             pltpu.VMEM((2, 4, 4, 4, BLOCK, QUARTER), bf16),
@@ -613,8 +651,8 @@
             dma((2,)),
             dma((2, 3)),
             dma((2, 3)),
-            dma((2, 3)),
-            dma((2, 3)),
+            dma((2, 4)),
+            dma((2, 4)),
             dma((8, 8)),
             dma((8, 8)),
             dma((4,)),
@@ -644,6 +682,8 @@
         mode_rates,
         skip_gain.reshape(TILES, LANES),
     )
+    tiles = tiles.reshape(ROWS // 8, TILES, 8, LANES).transpose(0, 2, 1, 3)
+    return tiles.reshape(ROWS, WIDE).astype(bf16)
 
 
 def solution(mesh):

time: 145 us -> 127 us (0.88)
  Pallas kernels: 143 us -> 124 us
  other arithmetic: 0 us -> 2.66 us
  local copies, waits for them, and re-layouts: 2.29 us -> 0 us
    pallas_call x1, Pallas kernels: 143 us -> 124 us  [per_device(): pl.pallas_call(operator_kernel, out_shape=jax.ShapeDtypeStruct((ROWS * TI...]
    convert_element_type x0 -> x1, other arithmetic: none -> 2.66 us  [per_device(): return tiles.reshape(ROWS, WIDE).astype(bf16)]
    unnamed x1 -> x0, local copies, waits for them, and re-layouts: 2.29 us -> none
where the time goes in v3:
time: 127 us
  Pallas kernels  124 us (98%)
  other arithmetic  2.66 us (2%)
    pallas_call x1, Pallas kernels, per_device(): pl.pallas_call(operator_kernel, out_shape=jax.ShapeDtypeStruct((ROWS * TI...  124 us
    convert_element_type x1, other arithmetic, per_device(): return tiles.reshape(ROWS, WIDE).astype(bf16)  2.66 us

profile of v3, /device:TPU:1, one launch (start us, length us, event | category | flops | bytes accessed | tf_op | source)
XLA Modules:
  0.0 127.0 jit_solution(15849508209063396425)
XLA Ops:
  0.0 124.3 %shard_map.91 = f32[4096,128]{1,0:T(8,128)} custom-call(bf16[128,4096]{1,0:T(8,128)(2,1)} %tokens.1, bf16[12,4096]{1,0:T(8,128)(2,1)} %bitcast.7, bf16[12,4096]{1,0:T(8,128)(2,1)} %pad_out.1, bf16[128,4096]{1,0:T(8,128)(2,1)} %query_in.1, bf16[128,4096]{1,0:T(8,128)(2,1)} %key_in.1, f32[3,7,4096]{2,1,0:T(8,128)} %short_taps.1, f32[16,4096]{1,0:T(8,128)} %residues.1, ...), custom_call_target="tpu_custom_call" | custom-call | tf_op jit(solution)/shard_map/pallas_call | solution.py:621
  124.3 2.7 %convert_element_type.12 = bf16[4096,128]{1,0:T(8,128)(2,1)} convert(f32[4096,128]{1,0:T(8,128)} %shard_map.91) | non-fusion elementwise | flops 524288 | bytes 3145728 | tf_op jit(solution)/shard_map/convert_element_type | solution.py:686

commit v4 on v3

--- a/solution.py
+++ b/solution.py
@@ -104,6 +104,7 @@
     deep_recv,
     ring_send,
     ring_recv,
+    piece_send,
     part_send,
     part_recv,
     swap_send,
@@ -206,7 +207,7 @@
         parts = [stage[f, i].astype(jnp.float32) for i in range(4)]
         weights[f, y, zh, x] = jnp.concatenate(parts, axis=0).astype(jnp.bfloat16)
 
-    def ring(axis, item, send_sems, recv_sems):
+    def ring(axis, item, send_sems, recv_sems, split=False):
         at = place[axis]
         plus, minus, far = step(at, 1), step(at, 3), step(at, 2)
 
@@ -217,16 +218,25 @@
             copy(ref, ref, send_sems(slot), recv_sems(slot), {axis: at}).wait_recv()
 
         def first():
-            out(item(at), 0, plus)
-            out(item(at), 1, minus)
+            if split:
+                out(item(at, 0), 0, plus)
+                out(item(at, 1), 1, minus)
+                out(item(at, 1), 4, plus)
+                out(item(at, 0), 5, minus)
+            else:
+                out(item(at), 0, plus)
+                out(item(at), 1, minus)
 
         def forward():
-            landed(item(minus), 0)
+            landed(item(minus, 0 if split else None), 0)
             out(item(minus, 0), 2, plus)
-            landed(item(plus), 1)
+            landed(item(plus, 1 if split else None), 1)
             out(item(plus, 1), 3, minus)
 
         def finish():
+            if split:
+                landed(item(minus, 1), 4)
+                landed(item(plus, 0), 5)
             landed(item(far, 0), 2)
             landed(item(far, 1), 3)
 
@@ -266,7 +276,23 @@
             item,
             lambda slot: ring_send.at[unit, base + slot],
             lambda slot: ring_recv.at[unit, base + slot],
-        )
+            late and unit >= 2,
+        )
+
+    def open_late(unit, by):
+        deep = zh
+        if unit == 0:
+            axis, piece = "y", weights.at[0, y, deep, step(x, by)]
+        else:
+            axis, piece = "x", weights.at[1, step(y, by), deep, x]
+        for slot, to in ((0, 1), (1, 3)):
+            send(
+                piece,
+                piece,
+                piece_send.at[unit, by, slot],
+                ring_recv.at[unit, 4 + slot],
+                {axis: step(place[axis], to)},
+            )
 
     deep = [deep_ring(f) for f in range(2)]
     early = [unit_ring(unit, False) for unit in range(8)]
@@ -327,6 +353,9 @@
         half, row = n // 8, n % 8
         return ref[half, pl.ds(group * 64 + row, 8, stride=8), :]
 
+    def state_of(ref, n, group):
+        return ref[group // 2, n // 8, pl.ds(group % 2 * 8 + n % 8, 8, stride=16), :]
+
     def at_group(group):
         return slice(group * 8, group * 8 + 8)
 
@@ -420,7 +449,7 @@
 
     def store_states(group, held):
         for n in range(MODES):
-            states[n // 8, pl.ds(group * 64 + n % 8, 8, stride=8), :] = held[n]
+            states[group // 2, n // 8, pl.ds(group % 2 * 8 + n % 8, 8, stride=16), :] = held[n]
 
     def summarize(group):
         store_states(group, run_modes(group, decays(group), 1, ROWS // 8, zeros))
@@ -429,7 +458,7 @@
         held = run_modes(group, decays(group), 0, 1, zeros)
         rest = [jnp.exp(-float(ROWS - 8) * mode_of(rate_rows, n, group)) for n in range(MODES)]
         store_states(
-            group, [mode_of(states, n, group) + rest[n] * held[n] for n in range(MODES)]
+            group, [state_of(states, n, group) + rest[n] * held[n] for n in range(MODES)]
         )
 
     def localize(group):
@@ -451,7 +480,7 @@
         rates = decays(group)
         skip = skip_gain[at_group(group), :]
         first = tuple(
-            mode_of(weight_rows, n, group) * mode_of(carried, n, group) for n in range(MODES)
+            mode_of(weight_rows, n, group) * state_of(carried, n, group) for n in range(MODES)
         )
 
         def advance(eight, held):
@@ -469,80 +498,110 @@
         lax.fori_loop(0, ROWS // 8, advance, first)
 
     def near_part(at):
-        return pl.ds(pl.multiple_of(at * 32, 32), 32)
-
-    def exchange_states():
+        return pl.ds(pl.multiple_of(at * 16, 16), 16)
+
+    def near_rates(half):
+        starts = [pl.multiple_of((2 * half + i) * 64 + near * 8, 8) for i in range(2)]
+        return jnp.concatenate([rate_rows[:, pl.ds(start, 8), :] for start in starts], axis=1)
+
+    def wait_all(buffer, sends, recvs, offsets, index):
+        for by in offsets:
+            came = buffer(index(by))
+            copy(came, came, sends.at[by - 1], recvs.at[by - 1], {"ch": ch}).wait_recv()
+
+    def send_near(half):
         for by in range(1, 8):
             to, device = near_device(by)
             send(
-                states.at[:, near_part(to)],
-                group_states.at[near],
-                near_send.at[by - 1],
-                near_recv.at[by - 1],
+                states.at[half, :, near_part(to)],
+                group_states.at[half, near],
+                near_send.at[half, by - 1],
+                near_recv.at[half, by - 1],
                 device,
             )
-        localize(0)
-        localize(1)
-        rate = rate_rows[:, near_part(near), :]
+
+    def send_across(buffer, slot, axis, half):
+        own = buffer.at[half, place[axis]]
+        for by in (2, 1, 3):
+            send(
+                own,
+                own,
+                scan_send.at[slot, half, by - 1],
+                scan_recv.at[slot, half, by - 1],
+                {axis: step(place[axis], by)},
+            )
+
+    def scan_across(buffer, slot, axis, half, decay):
+        at = place[axis]
+        wait_all(
+            lambda i: buffer.at[half, i],
+            scan_send.at[slot, half],
+            scan_recv.at[slot, half],
+            (1, 3, 2),
+            lambda by: step(at, 4 - by),
+        )
+        running = jnp.zeros(decay.shape, jnp.float32)
+        before = running
+        for k in range(4):
+            before = jnp.where(at == k, running, before)
+            running = decay * running + buffer[half, k]
+        return before, running
+
+    def before_near(by):
+        return lax.rem(near + 8 - by, 8)
+
+    def scan_near(half):
+        one = jnp.exp(-float(ROWS) * near_rates(half))
+        group_states[half, near] = states[half, :, near_part(near), :]
+        wait_all(
+            lambda i: group_states.at[half, i],
+            near_send.at[half],
+            near_recv.at[half],
+            range(1, 8),
+            before_near,
+        )
+        held = jnp.zeros(one.shape, jnp.float32)
+        for k in range(8):
+            group_before[half, k] = held
+            held = one * held + group_states[half, k]
+        deep_states[half, zh] = held
+        send_across(deep_states, 0, "zh", half)
+
+    def scan_deep(half):
+        decay = jnp.exp(-8.0 * ROWS * near_rates(half))
+        before, running = scan_across(deep_states, 0, "zh", half, decay)
+        wide_states[half, y] = running
+        send_across(wide_states, 1, "y", half)
+        return before
+
+    def scan_wide(half, deep_before):
+        rate = near_rates(half)
         one = jnp.exp(-float(ROWS) * rate)
-        eight = jnp.exp(-8.0 * ROWS * rate)
-        group_states[near] = states[:, near_part(near), :]
-        for by in range(1, 8):
-            came = group_states.at[lax.rem(near + 8 - by, 8)]
-            copy(came, came, near_send.at[by - 1], near_recv.at[by - 1], {"ch": ch}).wait_recv()
-        held = jnp.zeros(rate.shape, jnp.float32)
-        for k in range(8):
-            group_before[k] = held
-            held = one * held + group_states[k]
-
-        def across(buffer, axis, slot, own, decay, cover):
-            at = place[axis]
-            buffer[at] = own
-            for by in (1, 3, 2):
-                send(
-                    buffer.at[at],
-                    buffer.at[at],
-                    scan_send.at[slot, by - 1],
-                    scan_recv.at[slot, by - 1],
-                    {axis: step(at, by)},
-                )
-            cover()
-            for by in (1, 3, 2):
-                came = buffer.at[step(at, 4 - by)]
-                copy(
-                    came, came, scan_send.at[slot, by - 1], scan_recv.at[slot, by - 1], {"ch": ch}
-                ).wait_recv()
-            running = jnp.zeros(own.shape, jnp.float32)
-            before = running
-            for k in range(4):
-                before = jnp.where(at == k, running, before)
-                running = decay * running + buffer[k]
-            return before, running
-
-        deep_before, deep_total = across(
-            deep_states, "zh", 0, held, eight, lambda: (localize(2), localize(3))
-        )
-        wide_before, _ = across(
-            wide_states, "y", 1, deep_total, jnp.exp(-32.0 * ROWS * rate), lambda: None
-        )
+        wide_before, _ = scan_across(wide_states, 1, "y", half, jnp.exp(-32.0 * ROWS * rate))
         shift = jnp.exp(rate * (-8.0 * ROWS * zh.astype(jnp.float32)))
         entering = deep_before + shift * wide_before
         for k in range(8):
-            group_before[k] += entering
+            group_before[half, k] += entering
             entering = one * entering
         for by in range(1, 8):
             to, device = near_device(by)
             send(
-                group_before.at[to],
-                carried.at[:, near_part(near)],
-                back_send.at[by - 1],
-                back_recv.at[by - 1],
+                group_before.at[half, to],
+                carried.at[half, :, near_part(near)],
+                back_send.at[half, by - 1],
+                back_recv.at[half, by - 1],
                 device,
             )
-        carried[:, near_part(near), :] = group_before[near]
-        for by in range(1, 8):
-            came = carried.at[:, near_part(lax.rem(near + 8 - by, 8))]
-            copy(came, came, back_send.at[by - 1], back_recv.at[by - 1], {"ch": ch}).wait_recv()
+        carried[half, :, near_part(near), :] = group_before[half, near]
+
+    def wait_back(half):
+        wait_all(
+            lambda i: carried.at[half, :, near_part(i)],
+            back_send.at[half],
+            back_recv.at[half],
+            range(1, 8),
+            before_near,
+        )
 
     FIRST, FORWARD, FINISH = range(3)
 
@@ -554,14 +613,20 @@
     settle(0)
     early[0][FIRST]()
     deep[0][FIRST]()
+    open_late(0, 0)
     settle(1)
     early[1][FIRST]()
     deep[1][FIRST]()
-    both(early, 0, FORWARD)
+    open_late(1, 0)
+    for unit in (0, 1):
+        early[unit][FORWARD]()
+        open_late(unit, 1)
+        open_late(unit, 3)
     deep[0][FORWARD]()
     both(early, 1, FIRST)
-    both(early, 0, FINISH)
-    both(late, 0, FIRST)
+    for unit in (0, 1):
+        early[unit][FINISH]()
+        open_late(unit, 2)
     both(early, 1, FORWARD)
     deep[0][FINISH]()
     deep[1][FORWARD]()
@@ -601,14 +666,33 @@
     expand(2, False, True)
     gather_value()
     mix()
-    for group in range(GROUPS):
-        summarize(group)
+    summarize(0)
+    summarize(1)
     mix_first()
-    for group in range(GROUPS):
-        summarize_first(group)
-    exchange_states()
-    for group in range(GROUPS):
-        finish_group(group)
+    summarize_first(0)
+    summarize_first(1)
+    send_near(0)
+    summarize(2)
+    summarize(3)
+    summarize_first(2)
+    summarize_first(3)
+    send_near(1)
+    localize(0)
+    localize(1)
+    scan_near(0)
+    localize(2)
+    scan_near(1)
+    localize(3)
+    deep_before = [scan_deep(0)]
+    deep_before.append(scan_deep(1))
+    scan_wide(0, deep_before[0])
+    scan_wide(1, deep_before[1])
+    wait_back(0)
+    finish_group(0)
+    finish_group(1)
+    wait_back(1)
+    finish_group(2)
+    finish_group(3)
     for made in started:
         made.wait_send()
 
@@ -641,32 +725,33 @@
             pltpu.VMEM((ROWS, TILES, LANES), f32),
             pltpu.VMEM((ROWS, TILES, LANES), f32),
             pltpu.VMEM((ROWS, TILES, LANES), f32),
-            pltpu.VMEM((2, TILES * 8, LANES), f32),
-            pltpu.VMEM((2, TILES * 8, LANES), f32),
-            pltpu.VMEM((8, 2, 32, LANES), f32),
-            pltpu.VMEM((8, 2, 32, LANES), f32),
-            pltpu.VMEM((4, 2, 32, LANES), f32),
-            pltpu.VMEM((4, 2, 32, LANES), f32),
+            pltpu.VMEM((2, 2, TILES * 4, LANES), f32),
+            pltpu.VMEM((2, 2, TILES * 4, LANES), f32),
+            pltpu.VMEM((2, 8, 2, 16, LANES), f32),
+            pltpu.VMEM((2, 8, 2, 16, LANES), f32),
+            pltpu.VMEM((2, 4, 2, 16, LANES), f32),
+            pltpu.VMEM((2, 4, 2, 16, LANES), f32),
             dma,
             dma((2,)),
             dma((2, 3)),
             dma((2, 3)),
             dma((2, 4)),
             dma((2, 4)),
-            dma((8, 8)),
-            dma((8, 8)),
+            dma((8, 10)),
+            dma((8, 10)),
+            dma((2, 4, 2)),
             dma((4,)),
             dma((4,)),
             dma((4,)),
             dma((4,)),
             dma((3,)),
             dma((3,)),
-            dma((7,)),
-            dma((7,)),
-            dma((2, 3)),
-            dma((2, 3)),
-            dma((7,)),
-            dma((7,)),
+            dma((2, 7)),
+            dma((2, 7)),
+            dma((2, 2, 3)),
+            dma((2, 2, 3)),
+            dma((2, 7)),
+            dma((2, 7)),
         ],
         compiler_params=pltpu.CompilerParams(
             collective_id=0, has_side_effects=True, vmem_limit_bytes=60 * 2**20

time: 127 us -> 124 us (0.976)
  Pallas kernels: 124 us -> 121 us
    pallas_call x1, Pallas kernels: 124 us -> 121 us  [per_device(): pl.pallas_call(operator_kernel, out_shape=jax.ShapeDtypeStruct((ROWS * TI...]
where the time goes in v4:
time: 124 us; the launch traced here: 123 us
  Pallas kernels  121 us (98%)
  other arithmetic  2.66 us (2%)
    pallas_call x1, Pallas kernels, per_device(): pl.pallas_call(operator_kernel, out_shape=jax.ShapeDtypeStruct((ROWS * TI...  121 us
    convert_element_type x1, other arithmetic, per_device(): return tiles.reshape(ROWS, WIDE).astype(bf16)  2.66 us

profile of v4, /device:TPU:1, one launch (start us, length us, event | category | flops | bytes accessed | tf_op | source)
XLA Modules:
  0.0 123.5 jit_solution(9544278185694573505)
XLA Ops:
  0.0 120.8 %shard_map.91 = f32[4096,128]{1,0:T(8,128)} custom-call(bf16[128,4096]{1,0:T(8,128)(2,1)} %tokens.1, bf16[12,4096]{1,0:T(8,128)(2,1)} %bitcast.7, bf16[12,4096]{1,0:T(8,128)(2,1)} %pad_out.1, bf16[128,4096]{1,0:T(8,128)(2,1)} %query_in.1, bf16[128,4096]{1,0:T(8,128)(2,1)} %key_in.1, f32[3,7,4096]{2,1,0:T(8,128)} %short_taps.1, f32[16,4096]{1,0:T(8,128)} %residues.1, ...), custom_call_target="tpu_custom_call" | custom-call | tf_op jit(solution)/shard_map/pallas_call | solution.py:705
  120.8 2.7 %convert_element_type.12 = bf16[4096,128]{1,0:T(8,128)(2,1)} convert(f32[4096,128]{1,0:T(8,128)} %shard_map.91) | non-fusion elementwise | flops 524288 | bytes 3145728 | tf_op jit(solution)/shard_map/convert_element_type | solution.py:771

commit v5 on v4

--- a/solution.py
+++ b/solution.py
@@ -631,11 +631,11 @@
     deep[0][FINISH]()
     deep[1][FORWARD]()
     both(early, 2, FIRST)
-    deep[1][FINISH]()
-    prepare()
     both(late, 0, FORWARD)
     both(early, 1, FINISH)
     both(late, 1, FIRST)
+    prepare()
+    deep[1][FINISH]()
     both(early, 2, FORWARD)
     both(early, 3, FIRST)
     copy(tokens, chip_tokens.at[1], token_sems.at[0], token_sems.at[1], {"core": core}).wait_recv()
@@ -659,9 +659,9 @@
     expand(1, False, False)
     join(3)
     both(late, 3, FORWARD)
-    join(2)
     late[6][FINISH]()
     expand(3, False, False)
+    join(2)
     late[7][FINISH]()
     expand(2, False, True)
     gather_value()

time: 124 us -> 119 us (0.960)
  Pallas kernels: 121 us -> 116 us
    pallas_call x1, Pallas kernels: 121 us -> 116 us  [per_device(): pl.pallas_call(operator_kernel, out_shape=jax.ShapeDtypeStruct((ROWS * TI...]
where the time goes in v5:
time: 119 us
  Pallas kernels  116 us (97%)
  other arithmetic  2.66 us (2%)
    pallas_call x1, Pallas kernels, per_device(): pl.pallas_call(operator_kernel, out_shape=jax.ShapeDtypeStruct((ROWS * TI...  116 us
    convert_element_type x1, other arithmetic, per_device(): return tiles.reshape(ROWS, WIDE).astype(bf16)  2.66 us

profile of v5, /device:TPU:1, one launch (start us, length us, event | category | flops | bytes accessed | tf_op | source)
XLA Modules:
  0.0 119.0 jit_solution(12913550496313636930)
XLA Ops:
  0.0 116.4 %shard_map.91 = f32[4096,128]{1,0:T(8,128)} custom-call(bf16[128,4096]{1,0:T(8,128)(2,1)} %tokens.1, bf16[12,4096]{1,0:T(8,128)(2,1)} %bitcast.7, bf16[12,4096]{1,0:T(8,128)(2,1)} %pad_out.1, bf16[128,4096]{1,0:T(8,128)(2,1)} %query_in.1, bf16[128,4096]{1,0:T(8,128)(2,1)} %key_in.1, f32[3,7,4096]{2,1,0:T(8,128)} %short_taps.1, f32[16,4096]{1,0:T(8,128)} %residues.1, ...), custom_call_target="tpu_custom_call" | custom-call | tf_op jit(solution)/shard_map/pallas_call | solution.py:705
  116.4 2.7 %convert_element_type.12 = bf16[4096,128]{1,0:T(8,128)(2,1)} convert(f32[4096,128]{1,0:T(8,128)} %shard_map.91) | non-fusion elementwise | flops 524288 | bytes 3145728 | tf_op jit(solution)/shard_map/convert_element_type | solution.py:771

commit v6 on v5

--- a/solution.py
+++ b/solution.py
@@ -105,6 +105,8 @@
     ring_send,
     ring_recv,
     piece_send,
+    far_send,
+    far_recv,
     part_send,
     part_recv,
     swap_send,
@@ -207,7 +209,7 @@
         parts = [stage[f, i].astype(jnp.float32) for i in range(4)]
         weights[f, y, zh, x] = jnp.concatenate(parts, axis=0).astype(jnp.bfloat16)
 
-    def ring(axis, item, send_sems, recv_sems, split=False):
+    def ring(axis, item, send_sems, recv_sems, split=False, relayed=None):
         at = place[axis]
         plus, minus, far = step(at, 1), step(at, 3), step(at, 2)
 
@@ -229,18 +231,30 @@
 
         def forward():
             landed(item(minus, 0 if split else None), 0)
-            out(item(minus, 0), 2, plus)
+            if relayed is None:
+                out(item(minus, 0), 2, plus)
             landed(item(plus, 1 if split else None), 1)
-            out(item(plus, 1), 3, minus)
-
-        def finish():
+            if relayed is None:
+                out(item(plus, 1), 3, minus)
+
+        def finish_near():
             if split:
                 landed(item(minus, 1), 4)
                 landed(item(plus, 0), 5)
-            landed(item(far, 0), 2)
-            landed(item(far, 1), 3)
-
-        return first, forward, finish
+
+        def finish_far():
+            if relayed is None:
+                landed(item(far, 0), 2)
+                landed(item(far, 1), 3)
+            else:
+                came = item(far)
+                copy(came, came, far_send.at[relayed], far_recv.at[relayed], {axis: at}).wait_recv()
+
+        def finish():
+            finish_near()
+            finish_far()
+
+        return first, forward, finish, finish_near, finish_far
 
     def half_columns(half):
         return slice(None) if half is None else slice(half * 512, half * 512 + 512)
@@ -277,7 +291,14 @@
             lambda slot: ring_send.at[unit, base + slot],
             lambda slot: ring_recv.at[unit, base + slot],
             late and unit >= 2,
-        )
+            {5: 0, 6: 1}.get(unit) if late else None,
+        )
+
+    def relay_far():
+        column = weights.at[1, :, zh, step(x, 2)]
+        send(column, column, far_send.at[0], far_recv.at[0], {"zh": step(zh, 3)})
+        strip = weights.at[1, step(y, 2), zh]
+        send(strip, strip, far_send.at[1], far_recv.at[1], {"zh": step(zh, 1)})
 
     def open_late(unit, by):
         deep = zh
@@ -326,24 +347,28 @@
         copy(partial.at[r], theirs.at[r], part_send.at[r], part_recv.at[r], {"ch": ch}).wait_recv()
         low[r] = (partial[r] + theirs[r]).astype(jnp.bfloat16)
 
-    def expand(r, opening, closing):
+    def product(r, quarter):
+        return jnp.dot(
+            low[r], unit_weights(1, r, quarter), preferred_element_type=jnp.float32
+        ).reshape(2, ROWS, QUARTER)
+
+    def expand(r, opening):
         for quarter in range(4):
-            part = jnp.dot(
-                low[r], unit_weights(1, r, quarter), preferred_element_type=jnp.float32
-            ).reshape(2, ROWS, QUARTER)
             if opening:
-                total[:, quarter] = part
+                total[:, quarter] = product(r, quarter)
             else:
-                total[:, quarter] += part
-            if closing:
-                send(
-                    total.at[1, quarter],
-                    arrived.at[quarter],
-                    swap_send.at[quarter],
-                    swap_recv.at[quarter],
-                    {"core": 1 - core},
-                )
-
+                total[:, quarter] += product(r, quarter)
+
+    def close(r, by):
+        quarter = step(x, by)
+        total[:, quarter] += product(r, quarter)
+        send(
+            total.at[1, quarter],
+            arrived.at[quarter],
+            swap_send.at[by],
+            swap_recv.at[by],
+            {"core": 1 - core},
+        )
 
     def tap_of(branch, offset, group):
         start = (branch * TILES + group * 8) * 8 + offset
@@ -396,9 +421,9 @@
         filtered(1, keep_key)
 
     def gather_value():
-        for quarter in range(4):
-            came = arrived.at[quarter]
-            copy(came, came, swap_send.at[quarter], swap_recv.at[quarter], {"ch": ch}).wait_recv()
+        for by in range(4):
+            came = arrived.at[step(x, by)]
+            copy(came, came, swap_send.at[by], swap_recv.at[by], {"ch": ch}).wait_recv()
 
         def block_rows(pair):
             for tile in range(TILES):
@@ -603,7 +628,7 @@
             before_near,
         )
 
-    FIRST, FORWARD, FINISH = range(3)
+    FIRST, FORWARD, FINISH, NEAR, FAR = range(5)
 
     def both(rings, pair, action):
         for unit in (2 * pair, 2 * pair + 1):
@@ -641,6 +666,7 @@
     copy(tokens, chip_tokens.at[1], token_sems.at[0], token_sems.at[1], {"core": core}).wait_recv()
     both(late, 0, FINISH)
     project(0)
+    relay_far()
     both(late, 1, FORWARD)
     both(early, 2, FINISH)
     both(late, 2, FIRST)
@@ -648,22 +674,27 @@
     both(late, 1, FINISH)
     project(1)
     project(3)
-    join(0)
-    expand(0, True, False)
     both(late, 2, FORWARD)
     both(early, 3, FINISH)
     both(late, 3, FIRST)
-    both(late, 2, FINISH)
+    join(0)
+    expand(0, True)
+    late[4][FINISH]()
     project(2)
+    late[5][FINISH]()
     join(1)
-    expand(1, False, False)
+    expand(1, False)
+    both(late, 3, FORWARD)
     join(3)
-    both(late, 3, FORWARD)
     late[6][FINISH]()
-    expand(3, False, False)
+    expand(3, False)
     join(2)
-    late[7][FINISH]()
-    expand(2, False, True)
+    close(2, 0)
+    late[7][NEAR]()
+    close(2, 1)
+    close(2, 3)
+    late[7][FAR]()
+    close(2, 2)
     gather_value()
     mix()
     summarize(0)
@@ -740,6 +771,8 @@
             dma((8, 10)),
             dma((8, 10)),
             dma((2, 4, 2)),
+            dma((2,)),
+            dma((2,)),
             dma((4,)),
             dma((4,)),
             dma((4,)),

time: 119 us -> 117 us (0.983)
    pallas_call x1, Pallas kernels: 116 us -> 115 us  [per_device(): pl.pallas_call(operator_kernel, out_shape=jax.ShapeDtypeStruct((ROWS * TI...]
where the time goes in v6:
time: 117 us
  Pallas kernels  115 us (98%)
  other arithmetic  2.66 us (2%)
    pallas_call x1, Pallas kernels, per_device(): pl.pallas_call(operator_kernel, out_shape=jax.ShapeDtypeStruct((ROWS * TI...  115 us
    convert_element_type x1, other arithmetic, per_device(): return tiles.reshape(ROWS, WIDE).astype(bf16)  2.66 us

profile of v6, /device:TPU:1, one launch (start us, length us, event | category | flops | bytes accessed | tf_op | source)
XLA Modules:
  0.0 117.4 jit_solution(2742359456865421182)
XLA Ops:
  0.0 114.7 %shard_map.91 = f32[4096,128]{1,0:T(8,128)} custom-call(bf16[128,4096]{1,0:T(8,128)(2,1)} %tokens.1, bf16[12,4096]{1,0:T(8,128)(2,1)} %bitcast.7, bf16[12,4096]{1,0:T(8,128)(2,1)} %pad_out.1, bf16[128,4096]{1,0:T(8,128)(2,1)} %query_in.1, bf16[128,4096]{1,0:T(8,128)(2,1)} %key_in.1, f32[3,7,4096]{2,1,0:T(8,128)} %short_taps.1, f32[16,4096]{1,0:T(8,128)} %residues.1, ...), custom_call_target="tpu_custom_call" | custom-call | tf_op jit(solution)/shard_map/pallas_call | solution.py:736
  114.7 2.7 %convert_element_type.12 = bf16[4096,128]{1,0:T(8,128)(2,1)} convert(f32[4096,128]{1,0:T(8,128)} %shard_map.91) | non-fusion elementwise | flops 524288 | bytes 3145728 | tf_op jit(solution)/shard_map/convert_element_type | solution.py:804

commit v7 on v6

--- a/solution.py
+++ b/solution.py
@@ -18,7 +18,7 @@
 BLOCK = 48
 QUARTER = 1024
 RANKS = 12
-UNITS = ((0, 0), (1, 0), (0, 1), (0, 3), (0, 2), (1, 1), (1, 3), (1, 2))
+UNITS = ((0, 0), (1, 0), (0, 1), (0, 3), (0, 2), (1, 2), (1, 3), (1, 1))
 
 
 def lanes_of(tile):
@@ -291,7 +291,7 @@
             lambda slot: ring_send.at[unit, base + slot],
             lambda slot: ring_recv.at[unit, base + slot],
             late and unit >= 2,
-            {5: 0, 6: 1}.get(unit) if late else None,
+            {7: 0, 6: 1}.get(unit) if late else None,
         )
 
     def relay_far():
@@ -322,16 +322,22 @@
     def unit_weights(f, r, quarter):
         return weights[f, :, step(zh, r), quarter].reshape(4 * BLOCK, QUARTER)
 
+    def quarter_dot(rows_in, quarter):
+        columns = pl.ds(pl.multiple_of(quarter * QUARTER, QUARTER), QUARTER)
+        return lax.dot_general(
+            rows_in,
+            chip_tokens[:, :, columns].reshape(2 * ROWS, QUARTER),
+            (((1,), (1,)), ((), ())),
+            preferred_element_type=jnp.float32,
+        )
+
+    def send_part(ref, other, i):
+        send(ref, other, part_send.at[i], part_recv.at[i], {"ch": 1 - ch})
+
     def project(r):
         @pl.loop(0, 4)
         def _(quarter):
-            columns = pl.ds(pl.multiple_of(quarter * QUARTER, QUARTER), QUARTER)
-            part = lax.dot_general(
-                chip_tokens[:, :, columns].reshape(2 * ROWS, QUARTER),
-                unit_weights(0, r, quarter),
-                (((1,), (1,)), ((), ())),
-                preferred_element_type=jnp.float32,
-            )
+            part = quarter_dot(unit_weights(0, r, quarter), quarter)
 
             @pl.when(quarter == 0)
             def _():
@@ -341,15 +347,31 @@
             def _():
                 partial[r] += part
 
-        send(partial.at[r], theirs.at[r], part_send.at[r], part_recv.at[r], {"ch": 1 - ch})
+        send_part(partial.at[r], theirs.at[r], r)
+
+    def strip_of(by):
+        return pl.ds(pl.multiple_of(step(y, by) * BLOCK, BLOCK), BLOCK)
+
+    def project_strip(by):
+        strip = strip_of(by)
+        partial[2, strip, :] = summed(
+            [quarter_dot(weights[0, step(y, by), step(zh, 2), q], q) for q in range(4)]
+        )
+        send_part(partial.at[2, strip], theirs.at[2, strip], 4 + by)
 
     def join(r):
-        copy(partial.at[r], theirs.at[r], part_send.at[r], part_recv.at[r], {"ch": ch}).wait_recv()
+        for by in range(4) if r == 2 else (None,):
+            i = r if by is None else 4 + by
+            came = theirs.at[r] if by is None else theirs.at[r, strip_of(by)]
+            copy(came, came, part_send.at[i], part_recv.at[i], {"ch": ch}).wait_recv()
         low[r] = (partial[r] + theirs[r]).astype(jnp.bfloat16)
 
     def product(r, quarter):
-        return jnp.dot(
-            low[r], unit_weights(1, r, quarter), preferred_element_type=jnp.float32
+        return lax.dot_general(
+            low[r],
+            unit_weights(1, r, quarter),
+            (((0,), (0,)), ((), ())),
+            preferred_element_type=jnp.float32,
         ).reshape(2, ROWS, QUARTER)
 
     def expand(r, opening):
@@ -655,12 +677,13 @@
     both(early, 1, FORWARD)
     deep[0][FINISH]()
     deep[1][FORWARD]()
-    both(early, 2, FIRST)
+    early[4][FIRST]()
     both(late, 0, FORWARD)
     both(early, 1, FINISH)
+    deep[1][FINISH]()
+    early[5][FIRST]()
     both(late, 1, FIRST)
     prepare()
-    deep[1][FINISH]()
     both(early, 2, FORWARD)
     both(early, 3, FIRST)
     copy(tokens, chip_tokens.at[1], token_sems.at[0], token_sems.at[1], {"core": core}).wait_recv()
@@ -670,6 +693,7 @@
     both(late, 1, FORWARD)
     both(early, 2, FINISH)
     both(late, 2, FIRST)
+    project_strip(0)
     both(early, 3, FORWARD)
     both(late, 1, FINISH)
     project(1)
@@ -679,22 +703,25 @@
     both(late, 3, FIRST)
     join(0)
     expand(0, True)
-    late[4][FINISH]()
-    project(2)
+    late[4][NEAR]()
+    project_strip(1)
+    project_strip(3)
+    late[4][FAR]()
+    project_strip(2)
     late[5][FINISH]()
-    join(1)
-    expand(1, False)
+    join(3)
     both(late, 3, FORWARD)
-    join(3)
     late[6][FINISH]()
     expand(3, False)
     join(2)
-    close(2, 0)
+    expand(2, False)
+    join(1)
+    close(1, 0)
+    late[7][FAR]()
+    close(1, 2)
     late[7][NEAR]()
-    close(2, 1)
-    close(2, 3)
-    late[7][FAR]()
-    close(2, 2)
+    close(1, 1)
+    close(1, 3)
     gather_value()
     mix()
     summarize(0)
@@ -743,9 +770,9 @@
             pltpu.VMEM((2, ROWS, WIDE), bf16),
             pltpu.VMEM((2, 4, RANKS, QUARTER), bf16),
             pltpu.VMEM((2, 4, 4, 4, BLOCK, QUARTER), bf16),
-            pltpu.VMEM((4, 2 * ROWS, 4 * BLOCK), f32),
-            pltpu.VMEM((4, 2 * ROWS, 4 * BLOCK), f32),
-            pltpu.VMEM((4, 2 * ROWS, 4 * BLOCK), bf16),
+            pltpu.VMEM((4, 4 * BLOCK, 2 * ROWS), f32),
+            pltpu.VMEM((4, 4 * BLOCK, 2 * ROWS), f32),
+            pltpu.VMEM((4, 4 * BLOCK, 2 * ROWS), bf16),
             pltpu.VMEM((2, 4, ROWS, QUARTER), f32),
             pltpu.VMEM((4, ROWS, QUARTER), f32),
             pltpu.VMEM((3, 8, WIDE), bf16),
@@ -773,8 +800,8 @@
             dma((2, 4, 2)),
             dma((2,)),
             dma((2,)),
-            dma((4,)),
-            dma((4,)),
+            dma((8,)),
+            dma((8,)),
             dma((4,)),
             dma((4,)),
             dma((3,)),

time: 117 us -> 116 us (level)
  Pallas kernels: 115 us -> 113 us
    pallas_call x1, Pallas kernels: 115 us -> 113 us  [per_device(): pl.pallas_call(operator_kernel, out_shape=jax.ShapeDtypeStruct((ROWS * TI...]
where the time goes in v7:
time: 116 us
  Pallas kernels  113 us (97%)
  other arithmetic  2.66 us (2%)
    pallas_call x1, Pallas kernels, per_device(): pl.pallas_call(operator_kernel, out_shape=jax.ShapeDtypeStruct((ROWS * TI...  113 us
    convert_element_type x1, other arithmetic, per_device(): return tiles.reshape(ROWS, WIDE).astype(bf16)  2.66 us

profile of v7, /device:TPU:1, one launch (start us, length us, event | category | flops | bytes accessed | tf_op | source)
XLA Modules:
  0.0 116.2 jit_solution(12092090573847213119)
XLA Ops:
  0.0 113.5 %shard_map.91 = f32[4096,128]{1,0:T(8,128)} custom-call(bf16[128,4096]{1,0:T(8,128)(2,1)} %tokens.1, bf16[12,4096]{1,0:T(8,128)(2,1)} %bitcast.7, bf16[12,4096]{1,0:T(8,128)(2,1)} %pad_out.1, bf16[128,4096]{1,0:T(8,128)(2,1)} %query_in.1, bf16[128,4096]{1,0:T(8,128)(2,1)} %key_in.1, f32[3,7,4096]{2,1,0:T(8,128)} %short_taps.1, f32[16,4096]{1,0:T(8,128)} %residues.1, ...), custom_call_target="tpu_custom_call" | custom-call | tf_op jit(solution)/shard_map/pallas_call | solution.py:763
  113.5 2.7 %convert_element_type.12 = bf16[4096,128]{1,0:T(8,128)(2,1)} convert(f32[4096,128]{1,0:T(8,128)} %shard_map.91) | non-fusion elementwise | flops 524288 | bytes 3145728 | tf_op jit(solution)/shard_map/convert_element_type | solution.py:831

commit v8 on v7

--- a/solution.py
+++ b/solution.py
@@ -74,6 +74,7 @@
     skip_gain,
     out,
     last,
+    value_edges,
     chip_tokens,
     stage,
     weights,
@@ -113,6 +114,8 @@
     swap_recv,
     edge_send,
     edge_recv,
+    late_send,
+    late_recv,
     near_send,
     near_recv,
     scan_send,
@@ -404,10 +407,10 @@
         return ref[group // 2, n // 8, pl.ds(group % 2 * 8 + n % 8, 8, stride=16), :]
 
     def at_group(group):
-        return slice(group * 8, group * 8 + 8)
-
-    def filtered(branch, target, begin=0, end=ROWS // 8):
-        for group in range(GROUPS):
+        return pl.ds(group * 8 if isinstance(group, int) else pl.multiple_of(group * 8, 8), 8)
+
+    def filtered(branch, target, begin=0, end=ROWS // 8, groups=range(GROUPS)):
+        for group in groups:
             taps = [tap_of(branch, j, group) for j in range(TAPS)]
 
             @pl.loop(begin, end)
@@ -442,43 +445,51 @@
         spread(key_in, edges.at[1], first_block, rows)
         filtered(1, keep_key)
 
-    def gather_value():
+    def gather_rows(pair, quarter, edge):
+        where = pl.ds(pl.multiple_of(pair * 16, 16), 16)
+        for tile in range(8):
+            columns = lanes_of(tile)
+            block = total[0, quarter, where, columns] + arrived[quarter, where, columns]
+            block = block.astype(jnp.bfloat16)
+            if edge:
+                last[quarter, :, columns] = block[8:]
+            block = block.astype(jnp.float32)
+            base = pl.multiple_of((2 * pair + 1) * TILES * 8 + quarter * 64 + tile * 8, 8)
+            rows[pl.ds(base, 8), :] = block[:8]
+            rows[pl.ds(base + TILES * 8, 8), :] = block[8:]
+
+    def gather_edge(by):
+        quarter = step(x, by)
+        came = arrived.at[quarter]
+        copy(came, came, swap_send.at[by], swap_recv.at[by], {"ch": ch}).wait_recv()
+        gather_rows(ROWS // 16 - 1, quarter, True)
+        send(
+            last.at[quarter],
+            value_edges.at[quarter],
+            late_send.at[by],
+            late_recv.at[by],
+            block_device(1),
+        )
+
+    def keep_product(t, group, result):
+        product = mixed[t, at_group(group), :] * result
+        mixed[t, at_group(group), :] = product.astype(jnp.bfloat16).astype(jnp.float32)
+
+    def start_mix(by):
+        group = step(x, by)
+        pl.loop(0, ROWS // 16 - 1)(lambda pair: gather_rows(pair, group, False))
+        filtered(2, keep_product, 1, ROWS // 8, (group,))
+        summarize(group)
+
+    def mix_first():
+        from_x = block_device(127)["x"]
         for by in range(4):
-            came = arrived.at[step(x, by)]
-            copy(came, came, swap_send.at[by], swap_recv.at[by], {"ch": ch}).wait_recv()
-
-        def block_rows(pair):
-            for tile in range(TILES):
-                quarter, columns = tile // 8, lanes_of(tile % 8)
-                where = pl.ds(pl.multiple_of(pair * 16, 16), 16)
-                block = total[0, quarter, where, columns] + arrived[quarter, where, columns]
-                block = block.astype(jnp.bfloat16)
-                if isinstance(pair, int):
-                    last[:, lanes_of(tile)] = block[8:]
-                block = block.astype(jnp.float32)
-                base = pl.multiple_of((2 * pair + 1) * TILES * 8 + tile * 8, 8)
-                rows[pl.ds(base, 8), :] = block[:8]
-                rows[pl.ds(base + TILES * 8, 8), :] = block[8:]
-
-        block_rows(ROWS // 16 - 1)
-        send(last, edges.at[2], edge_send.at[2], edge_recv.at[2], block_device(1))
-        pl.loop(0, ROWS // 16 - 1)(block_rows)
-
-    def mix():
-        def keep(t, group, result):
-            product = mixed[t, at_group(group), :] * result
-            mixed[t, at_group(group), :] = product.astype(jnp.bfloat16).astype(jnp.float32)
-
-        filtered(2, keep, 1, ROWS // 8)
-
-    def mix_first():
-        def keep(t, group, result):
-            product = mixed[t, at_group(group), :] * result
-            mixed[t, at_group(group), :] = product.astype(jnp.bfloat16).astype(jnp.float32)
-
-        wait_edge(2)
-        spread_edge(edges.at[2], first_block, rows)
-        filtered(2, keep, 0, 1)
+            came = value_edges.at[step(from_x, by)]
+            copy(came, came, late_send.at[by], late_recv.at[by], {"ch": ch}).wait_recv()
+        for tile in range(TILES):
+            above = value_edges[tile // 8, :, lanes_of(tile % 8)].astype(jnp.float32)
+            rows[tile * 8 : tile * 8 + 8, :] = jnp.where(first_block, 0.0, above)
+        filtered(2, keep_product, 0, 1)
 
     def decays(group):
         return [jnp.exp(-mode_of(rate_rows, n, group)) for n in range(MODES)]
@@ -496,7 +507,8 @@
 
     def store_states(group, held):
         for n in range(MODES):
-            states[group // 2, n // 8, pl.ds(group % 2 * 8 + n % 8, 8, stride=16), :] = held[n]
+            half, part = lax.div(group, 2), lax.rem(group, 2)
+            states[half, n // 8, pl.ds(part * 8 + n % 8, 8, stride=16), :] = held[n]
 
     def summarize(group):
         store_states(group, run_modes(group, decays(group), 1, ROWS // 8, zeros))
@@ -711,27 +723,29 @@
     late[5][FINISH]()
     join(3)
     both(late, 3, FORWARD)
-    late[6][FINISH]()
-    expand(3, False)
     join(2)
     expand(2, False)
     join(1)
+    late[6][FINISH]()
+    expand(3, False)
     close(1, 0)
     late[7][FAR]()
     close(1, 2)
     late[7][NEAR]()
     close(1, 1)
     close(1, 3)
-    gather_value()
-    mix()
-    summarize(0)
-    summarize(1)
+    gather_edge(0)
+    gather_edge(2)
+    start_mix(0)
+    gather_edge(1)
+    gather_edge(3)
+    start_mix(2)
+    start_mix(1)
+    start_mix(3)
     mix_first()
     summarize_first(0)
     summarize_first(1)
     send_near(0)
-    summarize(2)
-    summarize(3)
     summarize_first(2)
     summarize_first(3)
     send_near(1)
@@ -766,7 +780,8 @@
         in_specs=[pl.BlockSpec(memory_space=pltpu.VMEM)] * 9,
         out_specs=pl.BlockSpec(memory_space=pltpu.VMEM),
         scratch_shapes=[
-            pltpu.VMEM((8, WIDE), bf16),
+            pltpu.VMEM((4, 8, QUARTER), bf16),
+            pltpu.VMEM((4, 8, QUARTER), bf16),
             pltpu.VMEM((2, ROWS, WIDE), bf16),
             pltpu.VMEM((2, 4, RANKS, QUARTER), bf16),
             pltpu.VMEM((2, 4, 4, 4, BLOCK, QUARTER), bf16),
@@ -775,7 +790,7 @@
             pltpu.VMEM((4, 4 * BLOCK, 2 * ROWS), bf16),
             pltpu.VMEM((2, 4, ROWS, QUARTER), f32),
             pltpu.VMEM((4, ROWS, QUARTER), f32),
-            pltpu.VMEM((3, 8, WIDE), bf16),
+            pltpu.VMEM((2, 8, WIDE), bf16),
             pltpu.VMEM(((ROWS + 8) * TILES, LANES), f32),
             pltpu.VMEM((3 * TILES * 8, LANES), f32),
             pltpu.VMEM((2, TILES * 8, LANES), f32),
@@ -804,8 +819,10 @@
             dma((8,)),
             dma((4,)),
             dma((4,)),
-            dma((3,)),
-            dma((3,)),
+            dma((2,)),
+            dma((2,)),
+            dma((4,)),
+            dma((4,)),
             dma((2, 7)),
             dma((2, 7)),
             dma((2, 2, 3)),

time: 116 us -> 115 us (level)
    pallas_call x1, Pallas kernels: 113 us -> 112 us  [per_device(): pl.pallas_call(operator_kernel, out_shape=jax.ShapeDtypeStruct((ROWS * TI...]
where the time goes in v8:
time: 115 us
  Pallas kernels  112 us (97%)
  other arithmetic  2.66 us (2%)
    pallas_call x1, Pallas kernels, per_device(): pl.pallas_call(operator_kernel, out_shape=jax.ShapeDtypeStruct((ROWS * TI...  112 us
    convert_element_type x1, other arithmetic, per_device(): return tiles.reshape(ROWS, WIDE).astype(bf16)  2.66 us

profile of v8, /device:TPU:1, one launch (start us, length us, event | category | flops | bytes accessed | tf_op | source)
XLA Modules:
  0.0 114.6 jit_solution(16658278923431808451)
XLA Ops:
  0.0 111.9 %shard_map.91 = f32[4096,128]{1,0:T(8,128)} custom-call(bf16[128,4096]{1,0:T(8,128)(2,1)} %tokens.1, bf16[12,4096]{1,0:T(8,128)(2,1)} %bitcast.7, bf16[12,4096]{1,0:T(8,128)(2,1)} %pad_out.1, bf16[128,4096]{1,0:T(8,128)(2,1)} %query_in.1, bf16[128,4096]{1,0:T(8,128)(2,1)} %key_in.1, f32[3,7,4096]{2,1,0:T(8,128)} %short_taps.1, f32[16,4096]{1,0:T(8,128)} %residues.1, ...), custom_call_target="tpu_custom_call" | custom-call | tf_op jit(solution)/shard_map/pallas_call | solution.py:777
  111.9 2.7 %convert_element_type.12 = bf16[4096,128]{1,0:T(8,128)(2,1)} convert(f32[4096,128]{1,0:T(8,128)} %shard_map.91) | non-fusion elementwise | flops 524288 | bytes 3145728 | tf_op jit(solution)/shard_map/convert_element_type | solution.py:848

commit v9 on v8

--- a/solution.py
+++ b/solution.py
@@ -66,13 +66,19 @@
     tokens,
     pad_in,
     pad_out,
+    query_far,
+    key_far,
+    taps_far,
+    residues_far,
+    rates_far,
+    skip_far,
+    out,
     query_in,
     key_in,
     short_taps,
     residues,
     mode_rates,
     skip_gain,
-    out,
     last,
     value_edges,
     chip_tokens,
@@ -98,6 +104,7 @@
     deep_states,
     wide_states,
     own_sem,
+    load_sems,
     token_sems,
     stage_send,
     stage_recv,
@@ -176,14 +183,29 @@
         edge = edges.at[i]
         copy(edge, edge, edge_send.at[i], edge_recv.at[i], {"ch": ch}).wait_recv()
 
+    own_copy = pltpu.make_async_copy(tokens, chip_tokens.at[0], own_sem)
+    own_copy.start()
+    loads = [
+        pltpu.make_async_copy(source, target, load_sems.at[i])
+        for i, (source, target) in enumerate(
+            (
+                (query_far, query_in),
+                (key_far, key_in),
+                (taps_far, short_taps),
+                (residues_far, residues),
+                (rates_far, mode_rates),
+                (skip_far, skip_gain),
+            )
+        )
+    ]
+    for load in loads:
+        load.start()
     barrier = pltpu.get_barrier_semaphore()
     greeted = [{"ch": 1 - ch}, block_device(1), block_device(127)]
     greeted += [near_device(by)[1] for by in range(1, 8)]
     greeted += [{axis: step(place[axis], by)} for axis in ("zh", "y") for by in (1, 2, 3)]
     for device in greeted:
         pl.semaphore_signal(barrier, inc=1, device_id=device, device_id_type=MESH)
-    own_copy = pltpu.make_async_copy(tokens, chip_tokens.at[0], own_sem)
-    own_copy.start()
     pl.semaphore_wait(barrier, len(greeted))
 
     for f in range(2):
@@ -197,8 +219,16 @@
                 stage_recv.at[f, by - 1],
                 {"x": to},
             )
-    send(tokens, chip_tokens.at[1], token_sems.at[0], token_sems.at[1], {"core": 1 - core})
+    own_copy.wait()
+    send(
+        chip_tokens.at[0],
+        chip_tokens.at[1],
+        token_sems.at[0],
+        token_sems.at[1],
+        {"core": 1 - core},
+    )
     for i, source in enumerate((query_in, key_in)):
+        loads[i].wait()
         send_edge(i, source)
 
     def settle(f):
@@ -420,6 +450,8 @@
                     target(eight * 8 + i, group, short(window, taps, i))
 
     def prepare():
+        for load in loads[2:]:
+            load.wait()
         for tile in range(TILES):
             for branch in range(3):
                 base = (branch * TILES + tile) * 8
@@ -668,7 +700,6 @@
         for unit in (2 * pair, 2 * pair + 1):
             rings[unit][action]()
 
-    own_copy.wait()
     settle(0)
     early[0][FIRST]()
     deep[0][FIRST]()
@@ -698,7 +729,7 @@
     prepare()
     both(early, 2, FORWARD)
     both(early, 3, FIRST)
-    copy(tokens, chip_tokens.at[1], token_sems.at[0], token_sems.at[1], {"core": core}).wait_recv()
+    copy(chip_tokens.at[0], chip_tokens.at[1], token_sems.at[0], token_sems.at[1], {"core": core}).wait_recv()
     both(late, 0, FINISH)
     project(0)
     relay_far()
@@ -777,9 +808,17 @@
     tiles = pl.pallas_call(
         operator_kernel,
         out_shape=jax.ShapeDtypeStruct((ROWS * TILES, LANES), f32),
-        in_specs=[pl.BlockSpec(memory_space=pltpu.VMEM)] * 9,
+        in_specs=[pl.BlockSpec(memory_space=pl.ANY)]
+        + [pl.BlockSpec(memory_space=pltpu.VMEM)] * 2
+        + [pl.BlockSpec(memory_space=pl.ANY)] * 6,
         out_specs=pl.BlockSpec(memory_space=pltpu.VMEM),
         scratch_shapes=[
+            pltpu.VMEM((ROWS, WIDE), bf16),
+            pltpu.VMEM((ROWS, WIDE), bf16),
+            pltpu.VMEM((3, TAPS, WIDE), f32),
+            pltpu.VMEM((MODES, WIDE), f32),
+            pltpu.VMEM((MODES, WIDE), f32),
+            pltpu.VMEM((TILES, LANES), f32),
             pltpu.VMEM((4, 8, QUARTER), bf16),
             pltpu.VMEM((4, 8, QUARTER), bf16),
             pltpu.VMEM((2, ROWS, WIDE), bf16),
@@ -805,6 +844,7 @@
             pltpu.VMEM((2, 4, 2, 16, LANES), f32),
             pltpu.VMEM((2, 4, 2, 16, LANES), f32),
             dma,
+            dma((6,)),
             dma((2,)),
             dma((2, 3)),
             dma((2, 3)),

time: 115 us -> 114 us (level)
  no operation moved by 1% of the time
where the time goes in v9:
time: 114 us
  Pallas kernels  111 us (97%)
  other arithmetic  2.66 us (2%)
    pallas_call x1, Pallas kernels, per_device(): pl.pallas_call(operator_kernel, out_shape=jax.ShapeDtypeStruct((ROWS * TI...  111 us
    convert_element_type x1, other arithmetic, per_device(): return tiles.reshape(ROWS, WIDE).astype(bf16)  2.66 us

profile of v9, /device:TPU:1, one launch (start us, length us, event | category | flops | bytes accessed | tf_op | source)
XLA Modules:
  0.0 113.9 jit_solution(10663486998159205114)
XLA Ops:
  0.0 111.2 %shard_map.91 = f32[4096,128]{1,0:T(8,128)} custom-call(bf16[128,4096]{1,0:T(8,128)(2,1)} %tokens.1, bf16[12,4096]{1,0:T(8,128)(2,1)} %bitcast.7, bf16[12,4096]{1,0:T(8,128)(2,1)} %pad_out.1, bf16[128,4096]{1,0:T(8,128)(2,1)} %query_far.1, bf16[128,4096]{1,0:T(8,128)(2,1)} %key_far.1, f32[3,7,4096]{2,1,0:T(8,128)} %taps_far.1, f32[16,4096]{1,0:T(8,128)} %residues_far.1, ...), custom_call_target="tpu_custom_call" | custom-call | tf_op jit(solution)/shard_map/pallas_call | solution.py:808
  111.2 2.7 %convert_element_type.12 = bf16[4096,128]{1,0:T(8,128)(2,1)} convert(f32[4096,128]{1,0:T(8,128)} %shard_map.91) | non-fusion elementwise | flops 524288 | bytes 3145728 | tf_op jit(solution)/shard_map/convert_element_type | solution.py:888

commit v10 on v9

--- a/solution.py
+++ b/solution.py
@@ -414,9 +414,9 @@
             else:
                 total[:, quarter] += product(r, quarter)
 
-    def close(r, by):
+    def close(units, by):
         quarter = step(x, by)
-        total[:, quarter] += product(r, quarter)
+        total[:, quarter] += summed([product(r, quarter) for r in units])
         send(
             total.at[1, quarter],
             arrived.at[quarter],
@@ -758,13 +758,12 @@
     expand(2, False)
     join(1)
     late[6][FINISH]()
-    expand(3, False)
-    close(1, 0)
+    close((3, 1), 0)
     late[7][FAR]()
-    close(1, 2)
+    close((3, 1), 2)
     late[7][NEAR]()
-    close(1, 1)
-    close(1, 3)
+    close((3, 1), 1)
+    close((3, 1), 3)
     gather_edge(0)
     gather_edge(2)
     start_mix(0)

time: 114 us -> 114 us (level)
  no operation moved by 1% of the time
where the time goes in v10:
time: 114 us; the launch traced here: 113 us
  Pallas kernels  111 us (97%)
  other arithmetic  2.66 us (2%)
    pallas_call x1, Pallas kernels, per_device(): pl.pallas_call(operator_kernel, out_shape=jax.ShapeDtypeStruct((ROWS * TI...  111 us
    convert_element_type x1, other arithmetic, per_device(): return tiles.reshape(ROWS, WIDE).astype(bf16)  2.66 us

profile of v10, /device:TPU:1, one launch (start us, length us, event | category | flops | bytes accessed | tf_op | source)
XLA Modules:
  0.0 113.4 jit_solution(10055248627032697935)
XLA Ops:
  0.0 110.7 %shard_map.91 = f32[4096,128]{1,0:T(8,128)} custom-call(bf16[128,4096]{1,0:T(8,128)(2,1)} %tokens.1, bf16[12,4096]{1,0:T(8,128)(2,1)} %bitcast.7, bf16[12,4096]{1,0:T(8,128)(2,1)} %pad_out.1, bf16[128,4096]{1,0:T(8,128)(2,1)} %query_far.1, bf16[128,4096]{1,0:T(8,128)(2,1)} %key_far.1, f32[3,7,4096]{2,1,0:T(8,128)} %taps_far.1, f32[16,4096]{1,0:T(8,128)} %residues_far.1, ...), custom_call_target="tpu_custom_call" | custom-call | tf_op jit(solution)/shard_map/pallas_call | solution.py:807
  110.7 2.7 %convert_element_type.12 = bf16[4096,128]{1,0:T(8,128)(2,1)} convert(f32[4096,128]{1,0:T(8,128)} %shard_map.91) | non-fusion elementwise | flops 524288 | bytes 3145728 | tf_op jit(solution)/shard_map/convert_element_type | solution.py:887
